TPU v7x, 256 devices: a whole 4x4x8 slice. The times are simulated.
256 devices in a mesh: energy: 32 (over x, z_hi, core), space: 8 (over y, z_lo).
Axes of the slice: x: 4, y: 4, z: 8 (z_hi: 4, z_lo: 2; z = z_hi * 2 + z_lo), core: 2. Of those that a mesh axis runs over, the one named last changes fastest.
Arguments:
- g_lesser: float32 [2, 256, 8, 256, 256], P(None, 'energy', 'space'), may hold values from -6 to 6
- g_greater: float32 [2, 256, 8, 256, 256], P(None, 'energy', 'space'), may hold values from -6 to 6
- v_diag: float32 [8, 256, 256], P('space'), may hold values from -0.375 to 0.375
- v_upper: float32 [8, 256, 256], P('space'), may hold values from -0.375 to 0.375
Outputs:
- screened: float32 [2, 64, 8, 256, 256], P(None, 'energy', 'space')
All inputs are finite; a program needn't handle non-finite values.
Results may differ from a plain program's by a relative error of at most 0.000098.
Values sent between devices are 32-bit elements; how exact they have to be, the bound alone decides.
No kernel may reach another device: no remote copies, remote signals or barrier semaphores. Data moves between devices by JAX's collectives and lax.ppermute only.
A program may use at most 128 MiB of HBM per device.

v0:
```python
import math

import jax
import jax.numpy as jnp
from jax import lax
from jax.sharding import PartitionSpec as P

NW = 64


prefactor = 0.0625


def extended(block, sides, width):
    for axis, dim in sides:
        count = lax.axis_size(axis)
        forward = [(i, i + 1) for i in range(count - 1)]
        backward = [(target, source) for source, target in forward]
        low = lax.ppermute(
            lax.slice_in_dim(block, block.shape[dim] - width, None, axis=dim), axis, forward
        )
        high = lax.ppermute(lax.slice_in_dim(block, 0, width, axis=dim), axis, backward)
        block = jnp.concatenate([low, block, high], axis=dim)
    return block


def from_behind(block, axis, distance):
    devices = range(lax.axis_size(axis))
    route = [(i - distance, i) for i in devices if i - distance in devices]
    return lax.ppermute(block, axis, route)


def tables(count):
    length = 2 * count
    freqs = jnp.arange(length, dtype=jnp.int32)[:, None]
    points = jnp.arange(count, dtype=jnp.int32)[None, :]
    phase = 2.0 * math.pi / length * (freqs * points % length).astype(jnp.float32)
    return (jnp.cos(phase), jnp.sin(phase))


def product(left, right):
    return jnp.dot(left, right, precision=lax.Precision.HIGHEST, preferred_element_type=jnp.float32)


def correlate(lesser, greater, keep):
    count = lesser.shape[1]
    rest = tuple(lesser.shape[2:])
    lesser = lesser.reshape(2, count, -1)
    greater = greater.reshape(2, count, -1)
    cosine, sine = tables(count)
    less_re = product(cosine, lesser[0]) + product(sine, lesser[1])
    less_im = product(cosine, lesser[1]) - product(sine, lesser[0])
    great_re = product(cosine, greater[0]) - product(sine, greater[1])
    great_im = product(cosine, greater[1]) + product(sine, greater[0])
    spec_re = less_re * great_re - less_im * great_im
    spec_im = less_re * great_im + less_im * great_re
    factor = prefactor / (2 * count)
    back_cos = cosine.T[:keep]
    back_sin = sine.T[:keep]
    out_re = (product(back_cos, spec_re) - product(back_sin, spec_im)) * factor
    out_im = (product(back_cos, spec_im) + product(back_sin, spec_re)) * factor
    return jnp.stack([out_re, out_im]).reshape((2, keep) + rest)


def sandwich(left, middle, right):
    halfway = jnp.einsum("rab,...rbd->...rad", left, middle, precision=lax.Precision.HIGHEST)
    return jnp.einsum("...rad,rdf->...raf", halfway, right, precision=lax.Precision.HIGHEST)


def local(g_lesser, g_greater, v_diag, v_upper):
    flipped = jnp.swapaxes(g_greater, 3, 4)
    less_entries, great_entries = (
        lax.all_to_all(g_lesser, "energy", split_axis=3, concat_axis=1, tiled=True),
        lax.all_to_all(flipped, "energy", split_axis=3, concat_axis=1, tiled=True),
    )
    polar_entries = correlate(less_entries, great_entries, NW)
    polar = lax.all_to_all(polar_entries, "energy", split_axis=1, concat_axis=3, tiled=True)
    padded = extended(polar, (("space", 2),), 1)
    upper_prev = from_behind(v_upper, "space", 1)
    uppers_before = jnp.concatenate([upper_prev, v_upper[:-1]], axis=0)
    own_term = sandwich(v_diag, polar, v_diag)
    above_term = sandwich(jnp.swapaxes(uppers_before, 1, 2), padded[:, :, :-2], uppers_before)
    below_term = sandwich(v_upper, padded[:, :, 2:], jnp.swapaxes(v_upper, 1, 2))
    return own_term + above_term + below_term


def solution(mesh):
    in_specs = (
        P(None, "energy", "space", None, None),
        P(None, "energy", "space", None, None),
        P("space", None, None),
        P("space", None, None),
    )
    out_specs = P(None, "energy", "space", None, None)
    return jax.shard_map(local, mesh=mesh, in_specs=in_specs, out_specs=out_specs, check_vma=False)
```

profile of v0, /device:TPU:8, one launch (start us, length us, event | category | flops | bytes accessed | tf_op | source)
XLA Modules:
  0.0 361.9 jit_solution(17413478167533312150)
XLA Ops:
  0.0 6.6 %copy.74 = f32[2,8,1,256,256]{4,1,2,0,3:T(8,128)} copy(f32[2,8,1,256,256]{4,3,2,1,0:T(8,128)} %param.4) | data formatting | bytes 8388608 | tf_op args[0]
  6.6 11.4 %all-to-all-start = ((f32[2,8,1,256,256]{4,1,2,0,3:T(8,128)}), f32[2,8,1,256,256]{4,1,2,0,3:T(8,128)}, u32[]{:S(2)}, u32[]{:S(2)}) async-start(f32[2,8,1,256,256]{4,1,2,0,3:T(8,128)} %copy.74), calls=%async_computation | async-start | bytes 8388608 | tf_op jit(solution)/shard_map/all_to_all | solution.py:73
  18.1 5.5 %copy.78 = f32[2,8,1,256,256]{3,1,0,2,4:T(8,128)} copy(f32[2,8,1,256,256]{4,3,2,1,0:T(8,128)} %param.5) | data formatting | bytes 8388608 | tf_op args[1]
  23.6 87.5 %all-to-all-done = f32[2,8,1,256,256]{4,1,2,0,3:T(8,128)} async-done(((f32[2,8,1,256,256]{4,1,2,0,3:T(8,128)}), f32[2,8,1,256,256]{4,1,2,0,3:T(8,128)}, u32[]{:S(2)}, u32[]{:S(2)}) %all-to-all-start) | async-done | bytes 4194336 | tf_op jit(solution)/shard_map/all_to_all | solution.py:73
  111.1 8.0 %all-to-all-start.1 = ((f32[2,8,1,256,256]{4,1,0,2,3:T(8,128)}), f32[2,8,1,256,256]{4,1,0,2,3:T(8,128)}, u32[]{:S(2)}, u32[]{:S(2)}) async-start(f32[2,8,1,256,256]{4,1,0,2,3:T(8,128)} %bitcast.134), calls=%async_computation.1 | async-start | bytes 8388608 | tf_op jit(solution)/shard_map/all_to_all | solution.py:74
  119.1 0.2 fusion.9
  119.3 4.6 %copy.119 = f32[2,8,1,256,256]{4,3,1,0,2:T(8,128)S(1)} copy(f32[2,8,1,256,256]{4,1,2,0,3:T(8,128)} %all-to-all-done) | data formatting | bytes 8388608 | tf_op jit(solution)/shard_map/all_to_all | solution.py:73
  124.0 0.4 fusion.75
  124.4 0.6 copy_bitcast_fusion.4
  125.0 0.9 copy.101
  125.9 0.9 copy.102
  126.7 5.7 %fusion.34 = f32[512,2048]{1,0:T(8,128)S(1)} fusion(f32[256,2048]{1,0:T(8,128)S(1)} %bitcast.132), kind=kOutput, calls=%fused_computation.58 | convolution fusion | flops 3223060480 | bytes 6291456 | tf_op jit(solution)/shard_map/dot_general | solution.py:42
  132.4 7.5 %fusion.30 = f32[512,2048]{1,0:T(8,128)} fusion(f32[256,2048]{1,0:T(8,128)S(1)} %bitcast.128), kind=kOutput, calls=%fused_computation.56 | convolution fusion | flops 3223060480 | bytes 6291456 | tf_op jit(solution)/shard_map/dot_general | solution.py:42
  139.9 7.2 %convolution_add_fusion.1 = f32[512,2048]{1,0:T(8,128)} fusion(f32[512,2048]{1,0:T(8,128)S(1)} %fusion.34, f32[256,2048]{1,0:T(8,128)S(1)} %bitcast.129), kind=kOutput, calls=%fused_computation.7 | convolution fusion | flops 3224109056 | bytes 10485760 | tf_op jit(solution)/shard_map/dot_general | solution.py:42
  147.1 50.9 %all-to-all-done.1 = f32[2,8,1,256,256]{4,1,0,2,3:T(8,128)} async-done(((f32[2,8,1,256,256]{4,1,0,2,3:T(8,128)}), f32[2,8,1,256,256]{4,1,0,2,3:T(8,128)}, u32[]{:S(2)}, u32[]{:S(2)}) %all-to-all-start.1) | async-done | bytes 4194336 | tf_op jit(solution)/shard_map/all_to_all | solution.py:74
  198.0 4.6 %copy.118 = f32[2,8,1,256,256]{4,3,1,0,2:T(8,128)S(1)} copy(f32[2,8,1,256,256]{4,1,0,2,3:T(8,128)} %all-to-all-done.1) | data formatting | bytes 8388608 | tf_op jit(solution)/shard_map/all_to_all | solution.py:74
  202.6 0.4 fusion.74
  203.0 0.6 copy_bitcast_fusion.2
  203.6 0.9 copy.103
  204.5 5.4 %fusion.32 = f32[512,2048]{1,0:T(8,128)S(1)} fusion(f32[256,2048]{1,0:T(8,128)S(1)} %bitcast.126), kind=kOutput, calls=%fused_computation.57 | convolution fusion | flops 3223060480 | bytes 6291456 | tf_op jit(solution)/shard_map/dot_general | solution.py:42
  210.0 0.9 copy.104
  210.8 5.6 %fusion.28 = f32[512,2048]{1,0:T(8,128)S(1)} fusion(f32[256,2048]{1,0:T(8,128)S(1)} %bitcast.130), kind=kOutput, calls=%fused_computation.55 | convolution fusion | flops 3223060480 | bytes 6291456 | tf_op jit(solution)/shard_map/dot_general | solution.py:42
  216.5 5.4 %convolution_subtract_fusion.1 = f32[512,2048]{1,0:T(8,128)S(1)} fusion(f32[512,2048]{1,0:T(8,128)S(1)} %fusion.32, f32[256,2048]{1,0:T(8,128)S(1)} %bitcast.131), kind=kOutput, calls=%fused_computation.6 | convolution fusion | flops 3224109056 | bytes 10485760 | tf_op jit(solution)/shard_map/dot_general | solution.py:42
  221.9 7.1 %convolution_add_fusion = f32[512,2048]{1,0:T(8,128)} fusion(f32[512,2048]{1,0:T(8,128)S(1)} %fusion.28, f32[256,2048]{1,0:T(8,128)S(1)} %bitcast.127), kind=kOutput, calls=%fused_computation.4 | convolution fusion | flops 3224109056 | bytes 10485760 | tf_op jit(solution)/shard_map/dot_general | solution.py:42
  229.1 8.8 %multiply_subtract_fusion = (f32[512,2048]{1,0:T(8,128)S(1)}, f32[512,2048]{1,0:T(8,128)S(1)}) fusion(f32[512,2048]{1,0:T(8,128)} %convolution_add_fusion, f32[512,2048]{1,0:T(8,128)S(1)} %copy-done.2, f32[512,2048]{1,0:T(8,128)S(1)} %convolution_subtract_fusion.1, f32[512,2048]{1,0:T(8,128)S(1)} %copy-done.1, f32[256,2048]{1,0:T(8,128)S(1)} %bitcast.133), kind=kOutput, calls=%fused_computation.3 | convolution fusion | flops 3230400512 | bytes 27262976 | tf_op jit(solution)/shard_map/dot_general | solution.py:42
  237.9 3.0 fusion.40
  240.9 3.0 fusion.41
  244.0 3.1 fusion.1
  247.0 0.2 copy.105
  247.2 3.1 fusion
  250.3 0.2 copy.106
  250.4 0.1 pad_maximum_fusion
  250.5 45.0 %all_to_all.48 = f32[2,64,1,8,256]{4,3,0,2,1:T(8,128)S(1)} all-to-all(f32[2,64,1,8,256]{4,3,0,2,1:T(8,128)S(1)} %pad_maximum_fusion), channel_id=1, replica_groups=mesh['energy'=32,'space'=8] {'energy'}, dimensions={1} | all-to-all | bytes 2097152 | tf_op jit(solution)/shard_map/all_to_all | solution.py:77
  295.6 0.1 copy.84
  295.7 0.1 copy.120
  295.8 0.3 copy.89
  296.1 0.0 copy-start.3
  296.1 8.9 %collective-permute-start.2 = (f32[2,2,1,256,256]{3,4,1,0,2:T(8,128)S(1)}, f32[2,2,1,256,256]{3,4,1,0,2:T(8,128)S(1)}, u32[]{:S(2)}, u32[]{:S(2)}) collective-permute-start(f32[2,2,1,256,256]{3,4,1,0,2:T(8,128)S(1)} %copy.89), channel_id=1, source_target_pairs={{1,0},{2,1},{3,2},{4,3},{5,4},{6,5},{7,6},{9,8},{10,9},{11,10},{12... | collective-permute-start | bytes 3145736 | tf_op jit(solution)/shard_map/ppermute | solution.py:22
  305.0 2.2 collective-permute-start
  307.2 4.8 %collective-permute-start.1 = (f32[1,256,256]{2,1,0:T(8,128)}, f32[1,256,256]{2,1,0:T(8,128)S(1)}, u32[]{:S(2)}, u32[]{:S(2)}) collective-permute-start(f32[1,256,256]{2,1,0:T(8,128)} %param.7), channel_id=1, source_target_pairs={{0,1},{1,2},{2,3},{3,4},{4,5},{5,6},{6,7},{8,9},{9,10},{10,11},{11... | collective-permute-start | bytes 786440 | tf_op jit(solution)/shard_map/ppermute | solution.py:30
  312.1 1.8 convolution_bitcast_fusion.2
  313.9 1.8 fusion.23
  315.7 13.4 %collective-permute-done.2 = f32[2,2,1,256,256]{3,4,1,0,2:T(8,128)S(1)} collective-permute-done((f32[2,2,1,256,256]{3,4,1,0,2:T(8,128)S(1)}, f32[2,2,1,256,256]{3,4,1,0,2:T(8,128)S(1)}, u32[]{:S(2)}, u32[]{:S(2)}) %collective-permute-start.2) | collective-permute-done | bytes 1048608 | tf_op jit(solution)/shard_map/ppermute | solution.py:22
  329.1 1.0 convolution_bitcast_fusion
  330.2 25.9 %collective-permute-done.1 = f32[1,256,256]{2,1,0:T(8,128)S(1)} collective-permute-done((f32[1,256,256]{2,1,0:T(8,128)}, f32[1,256,256]{2,1,0:T(8,128)S(1)}, u32[]{:S(2)}, u32[]{:S(2)}) %collective-permute-start.1) | collective-permute-done | bytes 262176 | tf_op jit(solution)/shard_map/ppermute | solution.py:30
  356.1 1.0 convolution_bitcast_fusion.1
  357.1 1.8 convolution_add_fusion.4
  358.9 2.8 fusion.2
  (8 shorter events, 0.0 us)
Async XLA Ops:
  0.0 312.1 %copy-start = (f32[1,256,256]{2,1,0:T(8,128)S(1)}, f32[1,256,256]{2,1,0:T(8,128)}, u32[]{:S(2)}) copy-start(f32[1,256,256]{2,1,0:T(8,128)} %param.6) | copy-start | bytes 786436
  6.6 104.4 %all-to-all-start = ((f32[2,8,1,256,256]{4,1,2,0,3:T(8,128)}), f32[2,8,1,256,256]{4,1,2,0,3:T(8,128)}, u32[]{:S(2)}, u32[]{:S(2)}) async-start(f32[2,8,1,256,256]{4,1,2,0,3:T(8,128)} %copy.74), calls=%async_computation | async-start | bytes 8388608 | tf_op jit(solution)/shard_map/all_to_all | solution.py:73
  111.1 87.0 %all-to-all-start.1 = ((f32[2,8,1,256,256]{4,1,0,2,3:T(8,128)}), f32[2,8,1,256,256]{4,1,0,2,3:T(8,128)}, u32[]{:S(2)}, u32[]{:S(2)}) async-start(f32[2,8,1,256,256]{4,1,0,2,3:T(8,128)} %bitcast.134), calls=%async_computation.1 | async-start | bytes 8388608 | tf_op jit(solution)/shard_map/all_to_all | solution.py:74
  221.9 7.1 %copy-start.1 = (f32[512,2048]{1,0:T(8,128)S(1)}, f32[512,2048]{1,0:T(8,128)}, u32[]{:S(2)}) copy-start(f32[512,2048]{1,0:T(8,128)} %fusion.30) | copy-start | bytes 12582916
  221.9 7.1 %copy-start.2 = (f32[512,2048]{1,0:T(8,128)S(1)}, f32[512,2048]{1,0:T(8,128)}, u32[]{:S(2)}) copy-start(f32[512,2048]{1,0:T(8,128)} %convolution_add_fusion.1) | copy-start | bytes 12582916
  296.1 33.0 %copy-start.3 = (f32[1,256,256]{2,1,0:T(8,128)S(1)}, f32[1,256,256]{2,1,0:T(8,128)}, u32[]{:S(2)}) copy-start(f32[1,256,256]{2,1,0:T(8,128)} %param.7) | copy-start | bytes 786436
  296.1 33.0 %collective-permute-start.2 = (f32[2,2,1,256,256]{3,4,1,0,2:T(8,128)S(1)}, f32[2,2,1,256,256]{3,4,1,0,2:T(8,128)S(1)}, u32[]{:S(2)}, u32[]{:S(2)}) collective-permute-start(f32[2,2,1,256,256]{3,4,1,0,2:T(8,128)S(1)} %copy.89), channel_id=1, source_target_pairs={{1,0},{2,1},{3,2},{4,3},{5,4},{6,5},{7,6},{9,8},{10,9},{11,10},{12... | collective-permute-start | bytes 3145736 | tf_op jit(solution)/shard_map/ppermute | solution.py:22
  305.0 51.1 %collective-permute-start = (f32[2,2,1,256,256]{3,4,1,0,2:T(8,128)S(1)}, f32[2,2,1,256,256]{3,4,1,0,2:T(8,128)S(1)}, u32[]{:S(2)}, u32[]{:S(2)}) collective-permute-start(f32[2,2,1,256,256]{3,4,1,0,2:T(8,128)S(1)} %copy.89), channel_id=1, source_target_pairs={{0,1},{1,2},{2,3},{3,4},{4,5},{5,6},{6,7},{8,9},{9,10},{10,11},{11... | collective-permute-start | bytes 3145736 | tf_op jit(solution)/shard_map/ppermute | solution.py:19
  307.2 48.8 %collective-permute-start.1 = (f32[1,256,256]{2,1,0:T(8,128)}, f32[1,256,256]{2,1,0:T(8,128)S(1)}, u32[]{:S(2)}, u32[]{:S(2)}) collective-permute-start(f32[1,256,256]{2,1,0:T(8,128)} %param.7), channel_id=1, source_target_pairs={{0,1},{1,2},{2,3},{3,4},{4,5},{5,6},{6,7},{8,9},{9,10},{10,11},{11... | collective-permute-start | bytes 786440 | tf_op jit(solution)/shard_map/ppermute | solution.py:30
where the time goes:
time: 366 us; the launch traced here: 362 us
  waiting for transfers between devices  178 us (49%)
  matrix products  75.2 us (21%)
  blocking collectives  45 us (12%)
  starting transfers between devices  35.4 us (10%)
  local copies, waits for them, and re-layouts  27.7 us (8%)
    all_to_all x1, waiting for transfers between devices, local(): lax.all_to_all(g_lesser, 'energy', split_axis=3, concat_axis=1, tiled=True)  87.5 us
    dot_general x12, matrix products, product(): jnp.dot(left, right, precision=lax.Precision.HIGHEST, preferred_element_t...  65 us
    all_to_all x1, waiting for transfers between devices, local(): lax.all_to_all(flipped, 'energy', split_axis=3, concat_axis=1, tiled=True)  50.9 us
    all_to_all x1, blocking collectives, local(): lax.all_to_all(polar_entries, 'energy', split_axis=1, concat_axis=3, tile...  45 us
    ppermute x1, waiting for transfers between devices, from_behind(): return lax.ppermute(block, axis, route)  25.9 us
    unnamed x18, local copies, waits for them, and re-layouts  17.2 us
    ppermute x1, waiting for transfers between devices, extended(): lax.ppermute(lax.slice_in_dim(block, 0, width, axis=dim), axis, backward)  13.4 us
    all_to_all x1, starting transfers between devices, local(): lax.all_to_all(g_lesser, 'energy', split_axis=3, concat_axis=1, tiled=True)  11.4 us
  transfers between devices with their start and end apart: 5, of which 4 were waited for; matrix products, arithmetic and copies ran while one was open for 11% of the time, Pallas kernels for 0%

commit v1 on v0

v1 whole, which is shorter than its diff:
```python
import numpy as np

import jax
import jax.numpy as jnp
from jax import lax
from jax.experimental import pallas as pl
from jax.experimental.layout import Layout, with_layout_constraint
from jax.experimental.pallas import tpu as pltpu
from jax.sharding import Mesh
from jax.sharding import PartitionSpec as P

NW = 64
PREFACTOR = 0.0625
CORES, PAIR = 2, 2
ENERGY = ("xz", "core")
SPACE = ("y", "zl")


def halves(table):
    high = table.astype(jnp.bfloat16)
    low = (table - high.astype(np.float64)).astype(jnp.bfloat16)
    return np.concatenate([high, high, low], axis=1)


def tables(block):
    length = 2 * block
    freqs = np.concatenate([np.arange(0, length, 2), np.arange(1, length, 2)])
    phase = 2.0 * np.pi / length * (np.outer(freqs, np.arange(block)) % length)
    c, s = np.cos(phase), np.sin(phase)
    lesser = np.block([[c, s], [-s, c]])
    greater = np.block([[c, -s], [s, c]])
    back = np.block([[c.T, -s.T], [s.T, c.T]]) * (PREFACTOR / length)
    return halves(lesser), halves(greater), halves(back)


def split(x):
    high = x.astype(jnp.bfloat16)
    low = (x - high.astype(jnp.float32)).astype(jnp.bfloat16)
    return high, low


def dot(left, right):
    return jnp.dot(left, right, preferred_element_type=jnp.float32)


def correlate_row(less_re, less_im, great_re, great_im, t_less, t_great, t_back):
    block = NW
    count = less_re.shape[0] // block
    parts = [split(x) for x in (less_re, less_im, great_re, great_im)]

    def spectrum(table, re, im, j):
        rows = slice(j * block, (j + 1) * block)
        high = [re[0][rows], im[0][rows]]
        low = [re[1][rows], im[1][rows]]
        return dot(table, jnp.concatenate(high + low + high, axis=0))

    acc_re = acc_im = None
    before = None
    for j in range(count):
        less = spectrum(t_less, parts[0], parts[1], j)
        great = spectrum(t_great, parts[2], parts[3], j)
        if before is None:
            w_re, w_im = great[: 2 * block], great[2 * block :]
        else:
            w_re = jnp.concatenate(
                [great[:block] + before[:block], great[block : 2 * block] - before[block : 2 * block]], axis=0
            )
            w_im = jnp.concatenate(
                [
                    great[2 * block : 3 * block] + before[2 * block : 3 * block],
                    great[3 * block :] - before[3 * block :],
                ],
                axis=0,
            )
        l_re, l_im = less[: 2 * block], less[2 * block :]
        re = l_re * w_re - l_im * w_im
        im = l_re * w_im + l_im * w_re
        acc_re = re if acc_re is None else acc_re + re
        acc_im = im if acc_im is None else acc_im + im
        before = great
    high, low = split(jnp.concatenate([acc_re, acc_im], axis=0))
    return dot(t_back, jnp.concatenate([high, low, high], axis=0))


def kernel(less_ref, great_ref, t_less, t_great, t_back, out_ref):
    energies = less_ref.shape[0] * less_ref.shape[3]
    columns = less_ref.shape[4]
    less = [less_ref[:, 0, c].reshape(energies, columns) for c in range(2)]
    great = [great_ref[:, 0, c].reshape(energies, columns) for c in range(2)]
    out = correlate_row(*less, *great, t_less[...], t_great[...], t_back[...])
    out_ref[0] = out.reshape(2, NW, columns)


def correlate(less, great):
    sources, rows, _, local, columns = less.shape
    consts = [jnp.asarray(t) for t in tables(NW)]
    spec = pl.BlockSpec((sources, 1, 2, local, columns), lambda i: (0, i, 0, 0, 0))
    fixed = [pl.BlockSpec(t.shape, lambda i: (0, 0)) for t in consts]
    return pl.pallas_call(
        kernel,
        grid=(rows,),
        in_specs=[spec, spec] + fixed,
        out_specs=pl.BlockSpec((1, 2, NW, columns), lambda i: (i, 0, 0, 0)),
        out_shape=jax.ShapeDtypeStruct((rows, 2, NW, columns), jnp.float32),
        compiler_params=pltpu.CompilerParams(
            dimension_semantics=("arbitrary",), vmem_limit_bytes=40 * 1024 * 1024
        ),
        cost_estimate=pl.CostEstimate(
            flops=4_000_000_000, bytes_accessed=9_500_000, transcendentals=0
        ),
    )(less, great, *consts)


def tripled(x, axis, order):
    parts = split(x)
    return jnp.concatenate([parts[i] for i in order], axis=axis)


def sandwich(left, middle, right):
    left = tripled(left, 1, (0, 0, 1))
    right = tripled(right, 0, (0, 1, 0))
    halfway = [dot(left, tripled(m, 0, (0, 1, 0))) for m in middle]
    return [dot(tripled(h, 1, (0, 0, 1)), right) for h in halfway]


def block_of(ref, *index):
    return ref[index].reshape(-1, ref.shape[-1])


def pair_kernel(even_ref, polar_ref, v0, v1, u0, u0_t, own_ref, send_ref):
    p0 = [block_of(polar_ref, slice(None), 0, c) for c in range(2)]
    p1 = [block_of(polar_ref, slice(None), 1, c) for c in range(2)]
    even = even_ref[0] == 1
    s0 = [x + y for x, y in zip(sandwich(v0[...], p0, v0[...]), sandwich(u0[...], p1, u0_t[...]))]
    s1 = [x + y for x, y in zip(sandwich(v1[...], p1, v1[...]), sandwich(u0_t[...], p0, u0[...]))]
    for c in range(2):
        own_ref[c] = jnp.where(even, s0[c], s1[c])
        send_ref[c] = jnp.where(even, s1[c], s0[c])


def outer_kernel(pick_ref, part_ref, before_ref, after_ref, left, right, out_ref):
    after = pick_ref[0] == 1
    p = [
        jnp.where(after, block_of(after_ref, slice(None), c), block_of(before_ref, slice(None), c))
        for c in range(2)
    ]
    term = sandwich(left[...], p, right[...])
    for c in range(2):
        out_ref[c] = part_ref[c] + term[c]


def on_core(body, outs, flops, scalars, *arrays):
    vmem = pl.BlockSpec(memory_space=pltpu.VMEM)
    smem = pl.BlockSpec(memory_space=pltpu.SMEM)
    size = sum(4 * x.size for x in arrays)
    return pl.pallas_call(
        body,
        in_specs=[smem] * len(scalars) + [vmem] * len(arrays),
        out_specs=[vmem] * len(outs),
        out_shape=outs,
        compiler_params=pltpu.CompilerParams(vmem_limit_bytes=40 * 1024 * 1024),
        cost_estimate=pl.CostEstimate(flops=flops, bytes_accessed=size, transcendentals=0),
    )(*scalars, *arrays)


SWAP = [(0, 1), (1, 0)]


def plain(x):
    return with_layout_constraint(x, Layout(major_to_minor=tuple(range(x.ndim))))


def local(g_lesser, g_greater, v_diag, v_upper):
    devices = lax.axis_size(ENERGY)
    size = g_lesser.shape[3]
    rows = size // devices
    length = lax.axis_size("y")
    forward = [(i, i + 1) for i in range(length - 1)]
    backward = [(j, i) for i, j in forward]

    def exchange(block):
        got = lax.all_to_all(block, ENERGY, split_axis=0, concat_axis=0, tiled=True)
        return got.reshape((devices, rows) + block.shape[1:])

    first_core = lax.axis_index("core") == 0
    even = lax.axis_index("zl") == 0
    v, u = v_diag[0], v_upper[0]
    theirs = lax.ppermute(jnp.where(first_core, v, u), "zl", SWAP)
    less_send, theirs = lax.optimization_barrier((g_lesser[:, :, 0].transpose(2, 0, 1, 3), theirs))
    less = exchange(less_send)

    other = lax.ppermute(theirs, "core", SWAP)
    v_pair = jnp.where(first_core, theirs, other)
    u_pair = jnp.where(first_core, other, theirs)
    v0, v1 = jnp.where(even, v, v_pair), jnp.where(even, v_pair, v)
    u0, u1 = jnp.where(even, u, u_pair), jnp.where(even, u_pair, u)
    u_before_t = lax.ppermute(u1, "y", forward).T
    own_left, send_left = jnp.where(even, u_before_t, u1), jnp.where(even, u1, u_before_t)

    great_send = g_greater[:, :, 0].transpose(3, 0, 1, 2)
    great_send, v0, v1, u0, u0_t, own_left, own_right, send_left, send_right = lax.optimization_barrier(
        (great_send, v0, v1, u0, u0.T, own_left, own_left.T, send_left, send_left.T)
    )
    great = exchange(great_send)

    polar = correlate(less, great)
    polar = lax.all_to_all(
        plain(polar.transpose(2, 1, 0, 3)), ENERGY + ("zl",), split_axis=0, concat_axis=0, tiled=True
    )
    polar = polar.reshape(devices, PAIR, 2, rows, size)
    p_before = lax.ppermute(polar[:, 1], "y", forward)
    p_after = lax.ppermute(polar[:, 0], "y", backward)

    flag = even.astype(jnp.int32).reshape(1)
    result = jax.ShapeDtypeStruct((2, size, size), jnp.float32)
    own, send = on_core(
        pair_kernel, [result, result], 3_200_000_000, [flag], polar, v0, v1, u0, u0_t
    )
    outer = (p_before, p_after)
    (send,) = on_core(
        outer_kernel, [result], 800_000_000, [flag], send, *outer, send_left, send_right
    )
    got = lax.ppermute(send, "zl", SWAP)
    (own,) = on_core(
        outer_kernel, [result], 800_000_000, [1 - flag], own, *outer, own_left, own_right
    )
    return jnp.stack([jnp.where(even, own, got), jnp.where(even, got, own)], axis=1)[:, :, None]


def solution(mesh):
    count, width = mesh.devices.shape
    fine = Mesh(
        mesh.devices.reshape(count // CORES, CORES, width // PAIR, PAIR), ENERGY + SPACE
    )
    blocks = P(None, ENERGY, SPACE, None, None)
    rows = P(SPACE, None, None)
    return jax.shard_map(
        local, mesh=fine, in_specs=(blocks, blocks, rows, rows), out_specs=blocks, check_vma=False
    )
```

time: 366 us -> 300 us (0.82)
  blocking collectives: 45 us -> 139 us
  waiting for transfers between devices: 178 us -> 102 us
  matrix products: 75.2 us -> 0 us
  Pallas kernels: 0 us -> 15.2 us
  starting transfers between devices: 35.4 us -> 23.3 us
  local copies, waits for them, and re-layouts: 27.7 us -> 19.5 us
    all_to_all x1 -> x2, blocking collectives: 45 us -> 139 us  [the longest x1 84.7 us: exchange(): got = lax.all_to_all(block, ENERGY, split_axis=0, concat_axis=0, tiled=True)]
    dot_general x18 -> x0, matrix products: 75.2 us -> none  [the longest x12 65 us: product(): jnp.dot(left, right, precision=lax.Precision.HIGHEST, preferred_element_t...]
    all_to_all x2 -> x1, waiting for transfers between devices: 138 us -> 80.7 us  [exchange(): got = lax.all_to_all(block, ENERGY, split_axis=0, concat_axis=0, tiled=True)]
    ppermute x3 -> x6, waiting for transfers between devices: 39.3 us -> 20.9 us  [the longest x1 8.66 us: local(): got = lax.ppermute(send, 'zl', SWAP)]
    pallas_call x0 -> x4, Pallas kernels: none -> 15.2 us  [the longest x1 9.77 us: correlate(): pl.pallas_call(kernel, grid=(rows,), in_specs=[spec, spec] + fixed, out_s...]
    all_to_all x5 -> x0, local copies, waits for them, and re-layouts: 9.73 us -> none  [the longest x1 4.62 us: local(): lax.all_to_all(g_lesser, 'energy', split_axis=3, concat_axis=1, tiled=True)]
    all_to_all x2 -> x1, starting transfers between devices: 19.5 us -> 11 us  [exchange(): got = lax.all_to_all(block, ENERGY, split_axis=0, concat_axis=0, tiled=True)]
    ppermute x3 -> x6, starting transfers between devices: 15.9 us -> 12.3 us  [the longest x1 3.48 us: local(): u_before_t = lax.ppermute(u1, 'y', forward).T]
  transfers between devices with their start and end apart: 5 -> 7, of which waited for: 4 -> 6; matrix products, arithmetic and copies ran while one was open for 11% -> 4% of each run, Pallas kernels for 0% -> 1%
where the time goes in v1:
time: 300 us; the launch traced here: 299 us
  blocking collectives  139 us (46%)
  waiting for transfers between devices  102 us (34%)
  starting transfers between devices  23.3 us (8%)
  local copies, waits for them, and re-layouts  19.5 us (6%)
  Pallas kernels  15.2 us (5%)
    all_to_all x1, blocking collectives, exchange(): got = lax.all_to_all(block, ENERGY, split_axis=0, concat_axis=0, tiled=True)  84.7 us
    all_to_all x1, waiting for transfers between devices, exchange(): got = lax.all_to_all(block, ENERGY, split_axis=0, concat_axis=0, tiled=True)  80.7 us
    all_to_all x1, blocking collectives, local(): lax.all_to_all(plain(polar.transpose(2, 1, 0, 3)), ENERGY + ('zl',), spli...  54.1 us
    unnamed x14, local copies, waits for them, and re-layouts  16 us
    all_to_all x1, starting transfers between devices, exchange(): got = lax.all_to_all(block, ENERGY, split_axis=0, concat_axis=0, tiled=True)  11 us
    pallas_call x1, Pallas kernels, correlate(): pl.pallas_call(kernel, grid=(rows,), in_specs=[spec, spec] + fixed, out_s...  9.77 us
    ppermute x1, waiting for transfers between devices, local(): got = lax.ppermute(send, 'zl', SWAP)  8.66 us
    ppermute x1, waiting for transfers between devices, local(): p_before = lax.ppermute(polar[:, 1], 'y', forward)  6.19 us
  transfers between devices with their start and end apart: 7, of which 6 were waited for; matrix products, arithmetic and copies ran while one was open for 4% of the time, Pallas kernels for 1%

profile of v1, /device:TPU:8, one launch (start us, length us, event | category | flops | bytes accessed | tf_op | source)
XLA Modules:
  0.0 298.9 jit_solution(4718532068792654741)
XLA Ops:
  0.0 1.1 copy.36
  1.1 1.1 copy.37
  2.2 2.0 collective-permute-start
  4.2 6.6 %copy.53 = f32[2,8,1,256,256]{4,1,0,3,2:T(8,128)} copy(f32[2,8,1,256,256]{4,3,2,1,0:T(8,128)} %param.7) | data formatting | bytes 8388608 | tf_op args[0]
  10.8 0.0 collective-permute-done
  10.8 11.0 %all-to-all-start = ((f32[256,2,8,256]{3,2,1,0:T(8,128)}), f32[256,2,8,256]{3,2,1,0:T(8,128)}, u32[]{:S(2)}, u32[]{:S(2)}) async-start(f32[256,2,8,256]{3,2,1,0:T(8,128)} %bitcast.49), calls=%async_computation | async-start | bytes 8388608 | tf_op jit(solution)/shard_map/all_to_all | solution.py:182
  21.8 0.3 collective-permute-start.1
  22.1 1.3 collective-permute-done.1
  23.4 0.1 bitcast_select_fusion.2
  23.5 3.5 %collective-permute-start.2 = (f32[256,256]{0,1:T(8,128)S(1)}, f32[256,256]{0,1:T(8,128)S(1)}, u32[]{:S(2)}, u32[]{:S(2)}) collective-permute-start(f32[256,256]{0,1:T(8,128)S(1)} %get-tuple-element.35), channel_id=1, source_target_pairs={{0,2},{2,4},{4,6},{1,3},{3,5},{5,7},{8,10},{10,12},{12,14},{9,11},... | collective-permute-start | bytes 786440 | tf_op jit(solution)/shard_map/ppermute | solution.py:197
  27.0 5.4 %copy.38 = f32[2,8,1,256,256]{3,1,0,4,2:T(8,128)} copy(f32[2,8,1,256,256]{4,3,2,1,0:T(8,128)} %param.8) | data formatting | bytes 8388608 | tf_op args[1]
  32.5 1.4 collective-permute-done.2
  33.8 0.1 copy.39
  34.0 0.0 copy-start
  34.0 0.0 copy-start.1
  34.0 0.0 copy-start.2
  34.1 80.7 %all-to-all-done = f32[256,2,8,256]{3,2,1,0:T(8,128)} async-done(((f32[256,2,8,256]{3,2,1,0:T(8,128)}), f32[256,2,8,256]{3,2,1,0:T(8,128)}, u32[]{:S(2)}, u32[]{:S(2)}) %all-to-all-start) | async-done | bytes 4194336 | tf_op jit(solution)/shard_map/all_to_all | solution.py:182
  114.8 84.7 %all_to_all.15 = f32[256,2,8,256]{3,2,1,0:T(8,128)S(1)} all-to-all(f32[256,2,8,256]{3,2,1,0:T(8,128)} %bitcast.50), channel_id=1, replica_groups=mesh['xz'=16,'core'=2,'y'=4,'zl'=2] {'xz','core'}, dimensions={0} | all-to-all | bytes 8388608 | tf_op jit(solution)/shard_map/all_to_all | solution.py:182
  199.4 0.0 copy-done
  199.4 0.0 copy-done.1
  199.4 0.0 copy-done.2
  199.5 9.8 %shard_map.73 = f32[8,2,64,256]{3,2,1,0:T(8,128)S(1)} custom-call(f32[32,8,2,8,256]{4,3,2,1,0:T(8,128)} %bitcast.5.less_ref, f32[32,8,2,8,256]{4,3,2,1,0:T(8,128)S(1)} %bitcast.43, bf16[256,384]{1,0:T(8,128)(2,1)S(1)} %copy-done, bf16[256,384]{1,0:T(8,128)(2,1)S(1)} %copy-done.1, bf16[128,768]{1,0:T(8,128)(2,1)S(1)} %copy-done.2), custom_call_target="tpu_custom_call" | custom-call | flops 4000000000 | bytes 9500000 | tf_op jit(solution)/shard_map/pallas_call | solution.py:99
  209.2 0.6 copy.54
  209.9 54.1 %all_to_all.16 = f32[64,2,8,256]{3,2,1,0:T(8,128)S(1)} all-to-all(f32[64,2,8,256]{3,2,1,0:T(8,128)S(1)} %bitcast.51), channel_id=1, replica_groups=mesh['xz'=16,'core'=2,'y'=4,'zl'=2] {'xz','core','zl'}, dimensions={0} | all-to-all | bytes 2097152 | tf_op jit(solution)/shard_map/all_to_all | solution.py:207
  263.9 1.1 slice_bitcast_fusion
  265.0 3.5 %collective-permute-start.3 = (f32[32,2,8,256]{3,2,1,0:T(8,128)}, f32[32,2,8,256]{3,2,1,0:T(8,128)S(1)}, u32[]{:S(2)}, u32[]{:S(2)}) collective-permute-start(f32[32,2,8,256]{3,2,1,0:T(8,128)} %get-tuple-element.34), channel_id=1, source_target_pairs={{0,2},{2,4},{4,6},{1,3},{3,5},{5,7},{8,10},{10,12},{12,14},{9,11},... | collective-permute-start | bytes 1572872 | tf_op jit(solution)/shard_map/ppermute | solution.py:211
  268.5 2.4 collective-permute-start.4
  270.9 0.1 copy.41.v0
  271.0 0.1 copy.42.v1
  271.1 0.1 copy.43.u0
  271.3 0.1 copy.47.left
  271.4 2.0 shard_map.74
  273.4 0.0 copy-start.3
  273.4 0.8 copy-done.3
  274.2 6.2 %collective-permute-done.3.before_ref = f32[32,2,8,256]{3,2,1,0:T(8,128)S(1)} collective-permute-done((f32[32,2,8,256]{3,2,1,0:T(8,128)}, f32[32,2,8,256]{3,2,1,0:T(8,128)S(1)}, u32[]{:S(2)}, u32[]{:S(2)}) %collective-permute-start.3) | collective-permute-done | bytes 524320 | tf_op jit(solution)/shard_map/ppermute | solution.py:211
  280.4 3.3 %collective-permute-done.4.after_ref = f32[32,2,8,256]{3,2,1,0:T(8,128)} collective-permute-done((f32[32,2,8,256]{3,2,1,0:T(8,128)}, f32[32,2,8,256]{3,2,1,0:T(8,128)}, u32[]{:S(2)}, u32[]{:S(2)}) %collective-permute-start.4) | collective-permute-done | bytes 524320 | tf_op jit(solution)/shard_map/ppermute | solution.py:212
  283.7 1.7 shard_map.76
  285.4 0.7 collective-permute-start.5
  286.1 0.1 copy.46.left
  286.3 0.0 copy-start.4
  286.3 1.0 copy-done.4
  287.3 1.7 shard_map.75
  289.0 8.7 %collective-permute-done.5 = f32[2,256,256]{2,1,0:T(8,128)S(1)} collective-permute-done((f32[2,256,256]{2,1,0:T(8,128)S(1)}, f32[2,256,256]{2,1,0:T(8,128)S(1)}, u32[]{:S(2)}, u32[]{:S(2)}) %collective-permute-start.5) | collective-permute-done | bytes 524320 | tf_op jit(solution)/shard_map/ppermute | solution.py:223
  297.7 0.1 select_bitcast_fusion.1
  297.8 0.1 maximum_bitcast_fusion
  297.9 1.0 copy.48
  (2 shorter events, 0.1 us)
Async XLA Ops:
  2.2 8.6 %collective-permute-start = (f32[256,256]{0,1:T(8,128)S(1)}, f32[256,256]{0,1:T(8,128)S(1)}, u32[]{:S(2)}, u32[]{:S(2)}) collective-permute-start(f32[256,256]{0,1:T(8,128)S(1)} %bitcast_select_fusion.4), channel_id=1, source_target_pairs={{0,1},{1,0},{2,3},{3,2},{4,5},{5,4},{6,7},{7,6},{8,9},{9,8},{10,11... | collective-permute-start | bytes 786440 | tf_op jit(solution)/shard_map/ppermute | solution.py:188
  10.8 104.0 %all-to-all-start = ((f32[256,2,8,256]{3,2,1,0:T(8,128)}), f32[256,2,8,256]{3,2,1,0:T(8,128)}, u32[]{:S(2)}, u32[]{:S(2)}) async-start(f32[256,2,8,256]{3,2,1,0:T(8,128)} %bitcast.49), calls=%async_computation | async-start | bytes 8388608 | tf_op jit(solution)/shard_map/all_to_all | solution.py:182
  21.8 1.6 collective-permute-start.1
  23.5 10.3 %collective-permute-start.2 = (f32[256,256]{0,1:T(8,128)S(1)}, f32[256,256]{0,1:T(8,128)S(1)}, u32[]{:S(2)}, u32[]{:S(2)}) collective-permute-start(f32[256,256]{0,1:T(8,128)S(1)} %get-tuple-element.35), channel_id=1, source_target_pairs={{0,2},{2,4},{4,6},{1,3},{3,5},{5,7},{8,10},{10,12},{12,14},{9,11},... | collective-permute-start | bytes 786440 | tf_op jit(solution)/shard_map/ppermute | solution.py:197
  34.0 165.4 %copy-start = (bf16[256,384]{1,0:T(8,128)(2,1)S(1)}, bf16[256,384]{1,0:T(8,128)(2,1)}, u32[]{:S(2)}) copy-start(bf16[256,384]{1,0:T(8,128)(2,1)} %constant.18.clone.t_less) | copy-start | bytes 589828
  34.0 165.4 %copy-start.1 = (bf16[256,384]{1,0:T(8,128)(2,1)S(1)}, bf16[256,384]{1,0:T(8,128)(2,1)}, u32[]{:S(2)}) copy-start(bf16[256,384]{1,0:T(8,128)(2,1)} %constant.19.clone.t_great) | copy-start | bytes 589828
  34.0 165.4 %copy-start.2 = (bf16[128,768]{1,0:T(8,128)(2,1)S(1)}, bf16[128,768]{1,0:T(8,128)(2,1)}, u32[]{:S(2)}) copy-start(bf16[128,768]{1,0:T(8,128)(2,1)} %constant.20.clone.t_back) | copy-start | bytes 589828
  265.0 15.4 %collective-permute-start.3 = (f32[32,2,8,256]{3,2,1,0:T(8,128)}, f32[32,2,8,256]{3,2,1,0:T(8,128)S(1)}, u32[]{:S(2)}, u32[]{:S(2)}) collective-permute-start(f32[32,2,8,256]{3,2,1,0:T(8,128)} %get-tuple-element.34), channel_id=1, source_target_pairs={{0,2},{2,4},{4,6},{1,3},{3,5},{5,7},{8,10},{10,12},{12,14},{9,11},... | collective-permute-start | bytes 1572872 | tf_op jit(solution)/shard_map/ppermute | solution.py:211
  268.5 15.2 %collective-permute-start.4 = (f32[32,2,8,256]{3,2,1,0:T(8,128)}, f32[32,2,8,256]{3,2,1,0:T(8,128)}, u32[]{:S(2)}, u32[]{:S(2)}) collective-permute-start(f32[32,2,8,256]{3,2,1,0:T(8,128)} %get-tuple-element.33), channel_id=1, source_target_pairs={{2,0},{4,2},{6,4},{3,1},{5,3},{7,5},{10,8},{12,10},{14,12},{11,9},... | collective-permute-start | bytes 1572872 | tf_op jit(solution)/shard_map/ppermute | solution.py:212
  273.4 0.8 copy-start.3
  285.4 12.2 %collective-permute-start.5 = (f32[2,256,256]{2,1,0:T(8,128)S(1)}, f32[2,256,256]{2,1,0:T(8,128)S(1)}, u32[]{:S(2)}, u32[]{:S(2)}) collective-permute-start(f32[2,256,256]{2,1,0:T(8,128)S(1)} %shard_map.76), channel_id=1, source_target_pairs={{0,1},{1,0},{2,3},{3,2},{4,5},{5,4},{6,7},{7,6},{8,9},{9,8},{10,11... | collective-permute-start | bytes 1572872 | tf_op jit(solution)/shard_map/ppermute | solution.py:223
  286.3 1.0 copy-start.4

commit v2 on v0

v2 whole, which is shorter than its diff:
```python
import functools

import numpy as np

import jax
import jax.numpy as jnp
from jax import lax
from jax.experimental import pallas as pl
from jax.experimental.layout import Layout, with_layout_constraint
from jax.experimental.pallas import tpu as pltpu
from jax.sharding import Mesh
from jax.sharding import PartitionSpec as P

NW = 64
LANES = 128
PREFACTOR = 0.0625
CORES, PAIR = 2, 2
ENERGY = ("xz", "core")
SPACE = ("y", "zl")


def cut(table):
    high = table.astype(jnp.bfloat16)
    return high, (table - high.astype(np.float64)).astype(jnp.bfloat16)


def tables(block):
    length = 2 * block
    freqs = np.concatenate([np.arange(0, block, 2), np.arange(1, block, 2)])
    odd = 2 * freqs + 1
    phase = np.pi / length * (np.outer(odd, np.arange(block)) % (2 * length))
    c, s = np.cos(phase), np.sin(phase)
    high, low = cut(np.concatenate([c, s], axis=0))
    there = np.concatenate([high, high, low, low], axis=1)
    high, low = cut(np.concatenate([c.T, s.T], axis=1) * (PREFACTOR / length))
    return there, np.concatenate([high, high, low], axis=1)


def split(x):
    high = x.astype(jnp.bfloat16)
    low = (x - high.astype(jnp.float32)).astype(jnp.bfloat16)
    return high, low


def dot(left, right):
    return jnp.dot(left, right, preferred_element_type=jnp.float32)


def spectrum(there, re, im, sign):
    both = split(jnp.concatenate([re, im], axis=1))
    sums = dot(there, jnp.concatenate([both[0], both[1], both[0], both[1]], axis=0))
    half, columns = sums.shape[0] // 2, re.shape[1]
    c_re, c_im = sums[:half, :columns], sums[:half, columns:]
    s_re, s_im = sums[half:, :columns], sums[half:, columns:]
    minus = (c_re - s_im, c_im + s_re)
    plus = (c_re + s_im, c_im - s_re)
    first, second = (plus, minus) if sign < 0 else (minus, plus)
    return tuple(jnp.concatenate([p, q], axis=0) for p, q in zip(first, second))


def shifted(now, before):
    n_re, n_im = now
    b_re, b_im = before
    quarter = n_re.shape[0] // 4
    re, im = [], []
    for part, sign in enumerate((1, -1, -1, 1)):
        rows = slice(part * quarter, (part + 1) * quarter)
        if sign > 0:
            re.append(n_re[rows] + b_im[rows])
            im.append(n_im[rows] - b_re[rows])
        else:
            re.append(n_re[rows] - b_im[rows])
            im.append(n_im[rows] + b_re[rows])
    return jnp.concatenate(re, axis=0), jnp.concatenate(im, axis=0)


def polar_row(less_re, less_im, great_re, great_im, there, back):
    re = im = before = None
    for j in range(great_re.shape[0] // NW):
        rows = slice(j * NW, (j + 1) * NW)
        great = spectrum(there, great_re[rows], great_im[rows], 1)
        w_re, w_im = great if before is None else shifted(great, before)
        l_re, l_im = spectrum(there, less_re[rows], less_im[rows], -1)
        p_re = l_re * w_re - l_im * w_im
        p_im = l_re * w_im + l_im * w_re
        re, im = (p_re, p_im) if re is None else (re + p_re, im + p_im)
        before = great
    half = NW
    real = jnp.concatenate([re[:half] + re[half:], im[half:] - im[:half]], axis=0)
    imag = jnp.concatenate([im[:half] + im[half:], re[:half] - re[half:]], axis=0)
    high, low = split(jnp.concatenate([real, imag], axis=1))
    out = dot(back, jnp.concatenate([high, low, high], axis=0))
    return out[:, : re.shape[1]], out[:, re.shape[1] :]


def polar_kernel(less_hbm, great_hbm, there, back, out_ref, held, sems):
    rows = held.shape[1]

    def copy(which, i):
        source = (less_hbm, great_hbm)[which]
        return pltpu.make_async_copy(source.at[:, i], held.at[which, i], sems.at[which, i])

    for i in range(rows):
        copy(0, i).start()
        copy(1, i).start()

    def row(i, carry):
        copy(0, i).wait()
        copy(1, i).wait()
        parts = [held[k, i, :, c].reshape(-1, held.shape[-1]) for k in range(2) for c in range(2)]
        for c, part in enumerate(polar_row(*parts, there[...], back[...])):
            wide = part.shape[1] // LANES
            for h in range(wide):
                place = pl.ds((c * wide + h) * rows + i, NW, stride=2 * wide * rows)
                out_ref[place, :] = part[:, h * LANES : (h + 1) * LANES]
        return carry

    lax.fori_loop(0, rows, row, 0)


def polar_of(less, great):
    sources, rows, _, local, columns = great.shape
    there, back = (jnp.asarray(t) for t in tables(NW))
    hbm = pl.BlockSpec(memory_space=pltpu.HBM)
    vmem = pl.BlockSpec(memory_space=pltpu.VMEM)
    out = pl.pallas_call(
        polar_kernel,
        in_specs=[hbm, hbm, vmem, vmem],
        out_specs=vmem,
        out_shape=jax.ShapeDtypeStruct((NW * 2 * rows * columns // LANES, LANES), jnp.float32),
        scratch_shapes=[
            pltpu.VMEM((2, rows, sources, 2, local, columns), jnp.float32),
            pltpu.SemaphoreType.DMA((2, rows)),
        ],
        compiler_params=pltpu.CompilerParams(vmem_limit_bytes=57 * 1024 * 1024),
        cost_estimate=pl.CostEstimate(
            flops=4_000_000_000, bytes_accessed=9_500_000, transcendentals=0
        ),
    )(less, great, there, back)
    return out.reshape(NW, 2, columns // LANES, rows, LANES)


def tripled(x, axis, order):
    parts = split(x)
    return jnp.concatenate([parts[i] for i in order], axis=axis)


def sandwich(left, middle, right):
    left = tripled(left, 1, (0, 0, 1))
    right = tripled(right, 0, (0, 1, 0))
    halfway = [dot(left, tripled(m, 0, (0, 1, 0))) for m in middle]
    return [dot(tripled(h, 1, (0, 0, 1)), right) for h in halfway]


def block_of(ref, *index):
    wide = ref.shape[-3]
    return jnp.concatenate([ref[(slice(None), *index, h)].reshape(-1, LANES) for h in range(wide)], axis=1)


def screen(near, far, outer, v, w, w_t, a, a_t):
    terms = (sandwich(v, near, v), sandwich(w, far, w_t), sandwich(a, outer, a_t))
    return [x + y + z for x, y, z in zip(*terms)]


def send_kernel(c, near, far, outer, v, w, w_t, a, a_t, out_ref):
    blocks = ([block_of(near, c)], [block_of(far, c)], [block_of(outer)])
    (out_ref[...],) = screen(*blocks, v[...], w[...], w_t[...], a[...], a_t[...])


def own_kernel(near, far, outer, v, w, w_t, a, a_t, out_ref):
    blocks = [[block_of(ref, c) for c in range(2)] for ref in (near, far, outer)]
    out_ref[0], out_ref[1] = screen(*blocks, v[...], w[...], w_t[...], a[...], a_t[...])


def on_core(body, shape, flops, *arrays):
    vmem = pl.BlockSpec(memory_space=pltpu.VMEM)
    return pl.pallas_call(
        body,
        in_specs=[vmem] * len(arrays),
        out_specs=vmem,
        out_shape=jax.ShapeDtypeStruct(shape, jnp.float32),
        compiler_params=pltpu.CompilerParams(vmem_limit_bytes=16 * 1024 * 1024),
        cost_estimate=pl.CostEstimate(
            flops=flops, bytes_accessed=sum(4 * x.size for x in arrays), transcendentals=0
        ),
    )(*arrays)


SWAP = [(0, 1), (1, 0)]


def plain(x):
    return with_layout_constraint(x, Layout(major_to_minor=tuple(range(x.ndim))))


def local(g_lesser, g_greater, v_diag, v_upper):
    devices = lax.axis_size(ENERGY)
    size = g_lesser.shape[3]
    rows = size // devices
    length = lax.axis_size("y")
    forward = [(i, i + 1) for i in range(length - 1)]

    first_core = lax.axis_index("core") == 0
    even = lax.axis_index("zl") == 0
    v, u = v_diag[0], v_upper[0]
    theirs = lax.ppermute(plain(jnp.where(first_core, v, u)), "zl", SWAP)
    less_send = g_lesser.reshape(2, -1, devices, rows, size).transpose(2, 0, 1, 3, 4)
    less_send, theirs = lax.optimization_barrier((plain(less_send), theirs))
    less = plain(lax.all_to_all(plain(less_send), ENERGY, split_axis=0, concat_axis=0, tiled=True))

    other = lax.ppermute(theirs, "core", SWAP)
    v_pair = jnp.where(first_core, theirs, other)
    u_pair = jnp.where(first_core, other, theirs)
    u0, u1 = jnp.where(even, u, u_pair), jnp.where(even, u_pair, u)
    before_t = plain(lax.ppermute(plain(u1), "y", forward)).T
    u0_t = u0.T
    w, w_t = jnp.where(even, u0_t, u0), jnp.where(even, u0, u0_t)
    sends, keeps = jnp.where(even, u1, before_t), jnp.where(even, before_t, u1)
    fixed = tuple(plain(x) for x in (v, v_pair, w, w_t, sends, sends.T, keeps, keeps.T))

    great_send = g_greater[:, :, 0].transpose(3, 0, 1, 2)
    great_send, fixed = lax.optimization_barrier((great_send, fixed))
    v_own, v_pair, w, w_t, sends, sends_t, keeps, keeps_t = fixed
    great = lax.all_to_all(great_send, ENERGY, split_axis=0, concat_axis=0, tiled=True)
    great = great.reshape((devices, rows) + great.shape[1:])

    polar = polar_of(plain(less.transpose(0, 3, 1, 2, 4)), great)
    polar = lax.all_to_all(
        plain(polar), ENERGY + ("zl",), split_axis=0, concat_axis=0, tiled=True
    )
    polar = polar.reshape((devices, PAIR) + polar.shape[1:])

    pair = [(i, l) for i in range(length) for l in range(PAIR)]
    number = {p: n for n, p in enumerate(pair)}
    toward, away = [], []
    for i, l in pair:
        step = 1 - 2 * l
        for route, target in ((toward, (i - step, l)), (away, (i + step, l))):
            if target in number:
                route.append((number[i, l], number[target]))
    near = plain(jnp.where(even, polar[:, 1], polar[:, 0]))
    far = plain(jnp.where(even, polar[:, 0], polar[:, 1]))
    for_send = [lax.ppermute(plain(far[:, c]), SPACE, toward) for c in range(2)]

    got = []
    for c in range(2):
        ready = on_core(
            functools.partial(send_kernel, c), (size, size), 600_000_000,
            near, far, for_send[c], v_pair, w, w_t, sends, sends_t,
        )
        if c == 0:
            ready, near_later = lax.optimization_barrier((ready, near))
            for_own = lax.ppermute(near_later, SPACE, away)
        got.append(plain(lax.ppermute(plain(ready), "zl", SWAP)))
    kept = on_core(
        own_kernel, (2, size, size), 1_200_000_000, far, near, for_own, v_own, w_t, w, keeps, keeps_t
    )
    out = []
    for c in range(2):
        out += [jnp.where(even, kept[c], got[c]), jnp.where(even, got[c], kept[c])]
    return plain(jnp.stack(out).reshape(2, PAIR, 1, size, size))


def solution(mesh):
    count, width = mesh.devices.shape
    fine = Mesh(
        mesh.devices.reshape(count // CORES, CORES, width // PAIR, PAIR), ENERGY + SPACE
    )
    blocks = P(None, ENERGY, SPACE, None, None)
    rows = P(SPACE, None, None)
    return jax.shard_map(
        local, mesh=fine, in_specs=(blocks, blocks, rows, rows), out_specs=blocks, check_vma=False
    )
```

time: 366 us -> 295 us (0.81)
  matrix products: 75.2 us -> 0 us
  Pallas kernels: 0 us -> 13.5 us
  local copies, waits for them, and re-layouts: 27.7 us -> 16.7 us
  blocking collectives: 45 us -> 53.7 us
  waiting for transfers between devices: 178 us -> 174 us
    dot_general x18 -> x0, matrix products: 75.2 us -> none  [the longest x12 65 us: product(): jnp.dot(left, right, precision=lax.Precision.HIGHEST, preferred_element_t...]
    ppermute x3 -> x8, waiting for transfers between devices: 39.3 us -> 21.3 us  [the longest x2 12.6 us: local(): for_send = [lax.ppermute(plain(far[:, c]), SPACE, toward) for c in range(2)]]
    all_to_all x2, waiting for transfers between devices: 138 us -> 153 us  [the longest x1 80.5 us: local(): lax.all_to_all(plain(less_send), ENERGY, split_axis=0, concat_axis=0, til...]
    pallas_call x0 -> x4, Pallas kernels: none -> 13.5 us  [the longest x1 9.55 us: polar_of(): pl.pallas_call(polar_kernel, in_specs=[hbm, hbm, vmem, vmem], out_specs=v...]
    unnamed x18 -> x5, local copies, waits for them, and re-layouts: 17.2 us -> 5.54 us
    all_to_all x5 -> x0, local copies, waits for them, and re-layouts: 9.73 us -> none  [the longest x1 4.62 us: local(): lax.all_to_all(g_lesser, 'energy', split_axis=3, concat_axis=1, tiled=True)]
    all_to_all x1, blocking collectives: 45 us -> 53.7 us  [local(): lax.all_to_all(plain(polar), ENERGY + ('zl',), split_axis=0, concat_axis=...]
    another operation x0 -> x2, local copies, waits for them, and re-layouts: none -> 5.97 us  [plain(): with_layout_constraint(x, Layout(major_to_minor=tuple(range(x.ndim))))]
  transfers between devices with their start and end apart: 5 -> 10, of which waited for: 4 -> 9; matrix products, arithmetic and copies ran while one was open for 11% -> 6% of each run, Pallas kernels for 0% -> 1%
where the time goes in v2:
time: 295 us; the launch traced here: 294 us
  waiting for transfers between devices  174 us (59%)
  blocking collectives  53.7 us (18%)
  starting transfers between devices  33.9 us (11%)
  local copies, waits for them, and re-layouts  16.7 us (6%)
  Pallas kernels  13.5 us (5%)
    all_to_all x1, waiting for transfers between devices, local(): lax.all_to_all(plain(less_send), ENERGY, split_axis=0, concat_axis=0, til...  80.5 us
    all_to_all x1, waiting for transfers between devices, local(): lax.all_to_all(great_send, ENERGY, split_axis=0, concat_axis=0, tiled=True)  72.2 us
    all_to_all x1, blocking collectives, local(): lax.all_to_all(plain(polar), ENERGY + ('zl',), split_axis=0, concat_axis=...  53.7 us
    ppermute x2, waiting for transfers between devices, local(): for_send = [lax.ppermute(plain(far[:, c]), SPACE, toward) for c in range(2)]  12.6 us
    all_to_all x1, starting transfers between devices, local(): lax.all_to_all(plain(less_send), ENERGY, split_axis=0, concat_axis=0, til...  11.3 us
    pallas_call x1, Pallas kernels, polar_of(): pl.pallas_call(polar_kernel, in_specs=[hbm, hbm, vmem, vmem], out_specs=v...  9.55 us
    all_to_all x1, starting transfers between devices, local(): lax.all_to_all(great_send, ENERGY, split_axis=0, concat_axis=0, tiled=True)  7.84 us
    another operation x2, local copies, waits for them, and re-layouts, plain(): with_layout_constraint(x, Layout(major_to_minor=tuple(range(x.ndim))))  5.97 us
  transfers between devices with their start and end apart: 10, of which 9 were waited for; matrix products, arithmetic and copies ran while one was open for 6% of the time, Pallas kernels for 1%

profile of v2, /device:TPU:8, one launch (start us, length us, event | category | flops | bytes accessed | tf_op | source)
XLA Modules:
  0.0 294.5 jit_solution(9929353761799575260)
XLA Ops:
  0.0 1.1 bitcast_select_fusion.6
  1.1 2.0 collective-permute-start
  3.1 4.8 %copy_bitcast_fusion.1 = f32[32,2,8,8,256]{4,3,2,1,0:T(8,128)} fusion(f32[2,8,1,256,256]{4,3,2,1,0:T(8,128)} %param.6), kind=kLoop, calls=%fused_computation.1 | loop fusion | bytes 8388608 | tf_op jit(solution)/shard_map/transpose | solution.py:207
  7.9 0.0 copy-start.1
  7.9 1.5 collective-permute-done
  9.4 11.3 %all-to-all-start = ((f32[32,2,8,8,256]{4,3,2,1,0:T(8,128)}), f32[32,2,8,8,256]{4,3,2,1,0:T(8,128)}, u32[]{:S(2)}, u32[]{:S(2)}) async-start(f32[32,2,8,8,256]{4,3,2,1,0:T(8,128)} %copy_bitcast_fusion.1), calls=%async_computation | async-start | bytes 8388608 | tf_op jit(solution)/shard_map/all_to_all | solution.py:209
  20.7 0.3 collective-permute-start.1
  20.9 1.3 collective-permute-done.1
  22.3 0.0 copy-done.1
  22.3 0.1 bitcast_select_fusion.4
  22.3 3.5 %collective-permute-start.2 = (f32[256,256]{1,0:T(8,128)S(1)}, f32[256,256]{1,0:T(8,128)S(1)}, u32[]{:S(2)}, u32[]{:S(2)}) collective-permute-start(f32[256,256]{1,0:T(8,128)S(1)} %get-tuple-element.37), channel_id=1, source_target_pairs={{0,2},{2,4},{4,6},{1,3},{3,5},{5,7},{8,10},{10,12},{12,14},{9,11},... | collective-permute-start | bytes 786440 | tf_op jit(solution)/shard_map/ppermute | solution.py:215
  25.8 5.5 %copy.28 = f32[2,8,1,256,256]{3,1,0,4,2:T(8,128)} copy(f32[2,8,1,256,256]{4,3,2,1,0:T(8,128)} %param.7) | data formatting | bytes 8388608 | tf_op args[1]
  31.4 0.1 copy.29
  31.6 1.1 collective-permute-done.2
  32.7 0.1 copy.30
  32.8 0.1 copy.31.a_t
  33.0 0.1 copy.32.a_t
  33.1 80.5 %all-to-all-done = f32[32,2,8,8,256]{4,3,2,1,0:T(8,128)} async-done(((f32[32,2,8,8,256]{4,3,2,1,0:T(8,128)}), f32[32,2,8,8,256]{4,3,2,1,0:T(8,128)}, u32[]{:S(2)}, u32[]{:S(2)}) %all-to-all-start) | async-done | bytes 4194336 | tf_op jit(solution)/shard_map/all_to_all | solution.py:209
  113.6 7.8 %all-to-all-start.1 = ((f32[256,2,8,256]{3,2,1,0:T(8,128)}), f32[256,2,8,256]{3,2,1,0:T(8,128)}, u32[]{:S(2)}, u32[]{:S(2)}) async-start(f32[256,2,8,256]{3,2,1,0:T(8,128)} %bitcast.76), calls=%async_computation.1 | async-start | bytes 8388608 | tf_op jit(solution)/shard_map/all_to_all | solution.py:224
  121.5 5.8 %copy.43 = f32[32,2,8,8,256]{4,2,1,3,0:T(8,128)} copy(f32[32,2,8,8,256]{4,3,2,1,0:T(8,128)} %all-to-all-done) | data formatting | bytes 8388608 | tf_op jit(solution)/shard_map/layout_constraint | solution.py:193
  127.3 72.2 %all-to-all-done.1 = f32[256,2,8,256]{3,2,1,0:T(8,128)} async-done(((f32[256,2,8,256]{3,2,1,0:T(8,128)}), f32[256,2,8,256]{3,2,1,0:T(8,128)}, u32[]{:S(2)}, u32[]{:S(2)}) %all-to-all-start.1) | async-done | bytes 4194336 | tf_op jit(solution)/shard_map/all_to_all | solution.py:224
  199.5 9.5 %shard_map.64 = f32[2048,128]{1,0:T(8,128)} custom-call(f32[32,8,2,8,256]{4,3,2,1,0:T(8,128)} %bitcast.78, f32[32,8,2,8,256]{4,3,2,1,0:T(8,128)} %bitcast.11.great_hbm, bf16[128,256]{1,0:T(8,128)(2,1)} %constant.14.clone.there, bf16[64,384]{1,0:T(8,128)(2,1)} %constant.15.clone.back), custom_call_target="tpu_custom_call" | custom-call | flops 4000000000 | bytes 9500000 | tf_op jit(solution)/shard_map/pallas_call | solution.py:126
  209.1 53.7 %all_to_all.15 = f32[64,2,2,8,128]{4,3,2,1,0:T(8,128)S(1)} all-to-all(f32[64,2,2,8,128]{4,3,2,1,0:T(8,128)} %bitcast.79), channel_id=1, replica_groups=mesh['xz'=16,'core'=2,'y'=4,'zl'=2] {'xz','core','zl'}, dimensions={0} | all-to-all | bytes 2097152 | tf_op jit(solution)/shard_map/all_to_all | solution.py:228
  262.8 0.0 copy-start
  262.8 0.1 select_bitcast_fusion.1
  262.9 2.4 collective-permute-start.3
  265.3 7.2 %collective-permute-done.3.outer = f32[32,2,8,128]{3,2,1,0:T(8,128)S(1)} collective-permute-done((f32[32,2,8,128]{3,2,1,0:T(8,128)S(1)}, f32[32,2,8,128]{3,2,1,0:T(8,128)S(1)}, u32[]{:S(2)}, u32[]{:S(2)}) %collective-permute-start.3) | collective-permute-done | bytes 262176 | tf_op jit(solution)/shard_map/ppermute | solution.py:243
  272.5 1.2 shard_map.65
  273.7 3.5 %collective-permute-start.4 = (f32[32,2,2,8,128]{4,3,2,1,0:T(8,128)S(1)}, f32[32,2,2,8,128]{4,3,2,1,0:T(8,128)S(1)}, u32[]{:S(2)}, u32[]{:S(2)}) collective-permute-start(f32[32,2,2,8,128]{4,3,2,1,0:T(8,128)S(1)} %get-tuple-element.26.near.far), channel_id=1, source_target_pairs={{0,2},{2,4},{3,1},{4,6},{5,3},{7,5},{8,10},{10,12},{11,9},{12,14},... | collective-permute-start | bytes 1572872 | tf_op jit(solution)/shard_map/ppermute | solution.py:253
  277.2 2.4 collective-permute-start.6
  279.6 0.7 collective-permute-start.5
  280.3 5.4 %collective-permute-done.6.outer = f32[32,2,8,128]{3,2,1,0:T(8,128)S(1)} collective-permute-done((f32[32,2,8,128]{3,2,1,0:T(8,128)S(1)}, f32[32,2,8,128]{3,2,1,0:T(8,128)S(1)}, u32[]{:S(2)}, u32[]{:S(2)}) %collective-permute-start.6) | collective-permute-done | bytes 262176 | tf_op jit(solution)/shard_map/ppermute | solution.py:243
  285.6 1.2 shard_map.67
  286.9 0.1 collective-permute-start.7
  287.0 1.1 collective-permute-done.4.outer
  288.1 0.0 copy-done
  288.1 1.6 shard_map.66
  289.6 0.0 collective-permute-done.5
  289.6 3.7 %collective-permute-done.7 = f32[256,256]{1,0:T(8,128)S(1)} collective-permute-done((f32[256,256]{1,0:T(8,128)S(1)}, f32[256,256]{1,0:T(8,128)S(1)}, u32[]{:S(2)}, u32[]{:S(2)}) %collective-permute-start.7) | collective-permute-done | bytes 262176 | tf_op jit(solution)/shard_map/ppermute | solution.py:254
  293.3 0.1 select_bitcast_fusion.5
  293.4 1.0 pad_maximum_fusion
  (3 shorter events, 0.1 us)
Async XLA Ops:
  1.1 8.3 %collective-permute-start = (f32[256,256]{1,0:T(8,128)S(1)}, f32[256,256]{1,0:T(8,128)S(1)}, u32[]{:S(2)}, u32[]{:S(2)}) collective-permute-start(f32[256,256]{1,0:T(8,128)S(1)} %bitcast_select_fusion.6), channel_id=1, source_target_pairs={{0,1},{1,0},{2,3},{3,2},{4,5},{5,4},{6,7},{7,6},{8,9},{9,8},{10,11... | collective-permute-start | bytes 786440 | tf_op jit(solution)/shard_map/ppermute | solution.py:206
  7.9 14.4 %copy-start.1 = (f32[1,256,256]{2,1,0:T(8,128)S(1)}, f32[1,256,256]{2,1,0:T(8,128)}, u32[]{:S(2)}) copy-start(f32[1,256,256]{2,1,0:T(8,128)} %param.9) | copy-start | bytes 786436
  9.4 104.2 %all-to-all-start = ((f32[32,2,8,8,256]{4,3,2,1,0:T(8,128)}), f32[32,2,8,8,256]{4,3,2,1,0:T(8,128)}, u32[]{:S(2)}, u32[]{:S(2)}) async-start(f32[32,2,8,8,256]{4,3,2,1,0:T(8,128)} %copy_bitcast_fusion.1), calls=%async_computation | async-start | bytes 8388608 | tf_op jit(solution)/shard_map/all_to_all | solution.py:209
  20.7 1.6 collective-permute-start.1
  22.3 10.3 %collective-permute-start.2 = (f32[256,256]{1,0:T(8,128)S(1)}, f32[256,256]{1,0:T(8,128)S(1)}, u32[]{:S(2)}, u32[]{:S(2)}) collective-permute-start(f32[256,256]{1,0:T(8,128)S(1)} %get-tuple-element.37), channel_id=1, source_target_pairs={{0,2},{2,4},{4,6},{1,3},{3,5},{5,7},{8,10},{10,12},{12,14},{9,11},... | collective-permute-start | bytes 786440 | tf_op jit(solution)/shard_map/ppermute | solution.py:215
  113.6 85.9 %all-to-all-start.1 = ((f32[256,2,8,256]{3,2,1,0:T(8,128)}), f32[256,2,8,256]{3,2,1,0:T(8,128)}, u32[]{:S(2)}, u32[]{:S(2)}) async-start(f32[256,2,8,256]{3,2,1,0:T(8,128)} %bitcast.76), calls=%async_computation.1 | async-start | bytes 8388608 | tf_op jit(solution)/shard_map/all_to_all | solution.py:224
  262.8 25.3 %copy-start = (f32[1,256,256]{2,1,0:T(8,128)S(1)}, f32[1,256,256]{2,1,0:T(8,128)}, u32[]{:S(2)}) copy-start(f32[1,256,256]{2,1,0:T(8,128)} %param.8) | copy-start | bytes 786436
  262.9 9.6 %collective-permute-start.3 = (f32[32,2,8,128]{3,2,1,0:T(8,128)S(1)}, f32[32,2,8,128]{3,2,1,0:T(8,128)S(1)}, u32[]{:S(2)}, u32[]{:S(2)}) collective-permute-start(f32[32,2,8,128]{3,2,1,0:T(8,128)S(1)} %get-tuple-element.41), channel_id=1, source_target_pairs={{1,3},{2,0},{3,5},{4,2},{5,7},{6,4},{9,11},{10,8},{11,13},{12,10},... | collective-permute-start | bytes 786440 | tf_op jit(solution)/shard_map/ppermute | solution.py:243
  273.7 14.3 %collective-permute-start.4 = (f32[32,2,2,8,128]{4,3,2,1,0:T(8,128)S(1)}, f32[32,2,2,8,128]{4,3,2,1,0:T(8,128)S(1)}, u32[]{:S(2)}, u32[]{:S(2)}) collective-permute-start(f32[32,2,2,8,128]{4,3,2,1,0:T(8,128)S(1)} %get-tuple-element.26.near.far), channel_id=1, source_target_pairs={{0,2},{2,4},{3,1},{4,6},{5,3},{7,5},{8,10},{10,12},{11,9},{12,14},... | collective-permute-start | bytes 1572872 | tf_op jit(solution)/shard_map/ppermute | solution.py:253
  277.2 8.4 %collective-permute-start.6 = (f32[32,2,8,128]{3,2,1,0:T(8,128)S(1)}, f32[32,2,8,128]{3,2,1,0:T(8,128)S(1)}, u32[]{:S(2)}, u32[]{:S(2)}) collective-permute-start(f32[32,2,8,128]{3,2,1,0:T(8,128)S(1)} %get-tuple-element.42), channel_id=1, source_target_pairs={{1,3},{2,0},{3,5},{4,2},{5,7},{6,4},{9,11},{10,8},{11,13},{12,10},... | collective-permute-start | bytes 786440 | tf_op jit(solution)/shard_map/ppermute | solution.py:243
  279.6 10.0 %collective-permute-start.5 = (f32[256,256]{1,0:T(8,128)S(1)}, f32[256,256]{1,0:T(8,128)S(1)}, u32[]{:S(2)}, u32[]{:S(2)}) collective-permute-start(f32[256,256]{1,0:T(8,128)S(1)} %shard_map.65), channel_id=1, source_target_pairs={{0,1},{1,0},{2,3},{3,2},{4,5},{5,4},{6,7},{7,6},{8,9},{9,8},{10,11... | collective-permute-start | bytes 786440 | tf_op jit(solution)/shard_map/ppermute | solution.py:254
  286.9 6.5 %collective-permute-start.7 = (f32[256,256]{1,0:T(8,128)S(1)}, f32[256,256]{1,0:T(8,128)S(1)}, u32[]{:S(2)}, u32[]{:S(2)}) collective-permute-start(f32[256,256]{1,0:T(8,128)S(1)} %shard_map.67), channel_id=1, source_target_pairs={{0,1},{1,0},{2,3},{3,2},{4,5},{5,4},{6,7},{7,6},{8,9},{9,8},{10,11... | collective-permute-start | bytes 786440 | tf_op jit(solution)/shard_map/ppermute | solution.py:254

commit v3 on v2

--- a/solution.py
+++ b/solution.py
@@ -10,6 +10,7 @@
 from jax.experimental.pallas import tpu as pltpu
 from jax.sharding import Mesh
 from jax.sharding import PartitionSpec as P
+
 
 NW = 64
 LANES = 128
@@ -240,7 +241,10 @@
                 route.append((number[i, l], number[target]))
     near = plain(jnp.where(even, polar[:, 1], polar[:, 0]))
     far = plain(jnp.where(even, polar[:, 0], polar[:, 1]))
-    for_send = [lax.ppermute(plain(far[:, c]), SPACE, toward) for c in range(2)]
+    for_send = []
+    for c in range(2):
+        for_send.append(lax.ppermute(plain(far[:, c]), SPACE, toward))
+    for_own = lax.ppermute(near, SPACE, away)
 
     got = []
     for c in range(2):
@@ -248,9 +252,6 @@
             functools.partial(send_kernel, c), (size, size), 600_000_000,
             near, far, for_send[c], v_pair, w, w_t, sends, sends_t,
         )
-        if c == 0:
-            ready, near_later = lax.optimization_barrier((ready, near))
-            for_own = lax.ppermute(near_later, SPACE, away)
         got.append(plain(lax.ppermute(plain(ready), "zl", SWAP)))
     kept = on_core(
         own_kernel, (2, size, size), 1_200_000_000, far, near, for_own, v_own, w_t, w, keeps, keeps_t

time: 295 us -> 288 us (0.976)
  waiting for transfers between devices: 174 us -> 166 us
    ppermute x3, waiting for transfers between devices: 13.7 us -> 5.22 us  [the longest x2 5.04 us: local(): for_send.append(lax.ppermute(plain(far[:, c]), SPACE, toward))]
where the time goes in v3:
time: 288 us; the launch traced here: 287 us
  waiting for transfers between devices  166 us (58%)
  blocking collectives  53.7 us (19%)
  starting transfers between devices  34.5 us (12%)
  local copies, waits for them, and re-layouts  16.7 us (6%)
  Pallas kernels  13.5 us (5%)
    all_to_all x1, waiting for transfers between devices, local(): lax.all_to_all(plain(less_send), ENERGY, split_axis=0, concat_axis=0, til...  80.5 us
    all_to_all x1, waiting for transfers between devices, local(): lax.all_to_all(great_send, ENERGY, split_axis=0, concat_axis=0, tiled=True)  72.2 us
    all_to_all x1, blocking collectives, local(): lax.all_to_all(plain(polar), ENERGY + ('zl',), split_axis=0, concat_axis=...  53.7 us
    all_to_all x1, starting transfers between devices, local(): lax.all_to_all(plain(less_send), ENERGY, split_axis=0, concat_axis=0, til...  11.3 us
    pallas_call x1, Pallas kernels, polar_of(): pl.pallas_call(polar_kernel, in_specs=[hbm, hbm, vmem, vmem], out_specs=v...  9.55 us
    all_to_all x1, starting transfers between devices, local(): lax.all_to_all(great_send, ENERGY, split_axis=0, concat_axis=0, tiled=True)  7.84 us
    another operation x2, local copies, waits for them, and re-layouts, plain(): with_layout_constraint(x, Layout(major_to_minor=tuple(range(x.ndim))))  5.97 us
  transfers between devices with their start and end apart: 10, of which 9 were waited for; matrix products, arithmetic and copies ran while one was open for 6% of the time, Pallas kernels for 1%

profile of v3, /device:TPU:8, one launch (start us, length us, event | category | flops | bytes accessed | tf_op | source)
XLA Modules:
  0.0 287.4 jit_solution(18239776287335140312)
XLA Ops:
  0.0 1.1 bitcast_select_fusion.6
  1.1 2.0 collective-permute-start
  3.1 4.8 %copy_bitcast_fusion.1 = f32[32,2,8,8,256]{4,3,2,1,0:T(8,128)} fusion(f32[2,8,1,256,256]{4,3,2,1,0:T(8,128)} %param.6), kind=kLoop, calls=%fused_computation.1 | loop fusion | bytes 8388608 | tf_op jit(solution)/shard_map/transpose | solution.py:208
  7.9 0.0 copy-start.1
  7.9 1.5 collective-permute-done
  9.4 11.3 %all-to-all-start = ((f32[32,2,8,8,256]{4,3,2,1,0:T(8,128)}), f32[32,2,8,8,256]{4,3,2,1,0:T(8,128)}, u32[]{:S(2)}, u32[]{:S(2)}) async-start(f32[32,2,8,8,256]{4,3,2,1,0:T(8,128)} %copy_bitcast_fusion.1), calls=%async_computation | async-start | bytes 8388608 | tf_op jit(solution)/shard_map/all_to_all | solution.py:210
  20.7 0.3 collective-permute-start.1
  20.9 1.3 collective-permute-done.1
  22.3 0.0 copy-done.1
  22.3 0.1 bitcast_select_fusion.4
  22.3 3.5 %collective-permute-start.2 = (f32[256,256]{1,0:T(8,128)S(1)}, f32[256,256]{1,0:T(8,128)S(1)}, u32[]{:S(2)}, u32[]{:S(2)}) collective-permute-start(f32[256,256]{1,0:T(8,128)S(1)} %get-tuple-element.33), channel_id=1, source_target_pairs={{0,2},{2,4},{4,6},{1,3},{3,5},{5,7},{8,10},{10,12},{12,14},{9,11},... | collective-permute-start | bytes 786440 | tf_op jit(solution)/shard_map/ppermute | solution.py:216
  25.8 5.5 %copy.28 = f32[2,8,1,256,256]{3,1,0,4,2:T(8,128)} copy(f32[2,8,1,256,256]{4,3,2,1,0:T(8,128)} %param.7) | data formatting | bytes 8388608 | tf_op args[1]
  31.4 0.1 copy.29
  31.6 1.1 collective-permute-done.2
  32.7 0.1 copy.30
  32.8 0.1 copy.31.a_t
  33.0 0.1 copy.32.a_t
  33.1 80.5 %all-to-all-done = f32[32,2,8,8,256]{4,3,2,1,0:T(8,128)} async-done(((f32[32,2,8,8,256]{4,3,2,1,0:T(8,128)}), f32[32,2,8,8,256]{4,3,2,1,0:T(8,128)}, u32[]{:S(2)}, u32[]{:S(2)}) %all-to-all-start) | async-done | bytes 4194336 | tf_op jit(solution)/shard_map/all_to_all | solution.py:210
  113.6 7.8 %all-to-all-start.1 = ((f32[256,2,8,256]{3,2,1,0:T(8,128)}), f32[256,2,8,256]{3,2,1,0:T(8,128)}, u32[]{:S(2)}, u32[]{:S(2)}) async-start(f32[256,2,8,256]{3,2,1,0:T(8,128)} %bitcast.76), calls=%async_computation.1 | async-start | bytes 8388608 | tf_op jit(solution)/shard_map/all_to_all | solution.py:225
  121.5 5.8 %copy.43 = f32[32,2,8,8,256]{4,2,1,3,0:T(8,128)} copy(f32[32,2,8,8,256]{4,3,2,1,0:T(8,128)} %all-to-all-done) | data formatting | bytes 8388608 | tf_op jit(solution)/shard_map/layout_constraint | solution.py:194
  127.3 72.2 %all-to-all-done.1 = f32[256,2,8,256]{3,2,1,0:T(8,128)} async-done(((f32[256,2,8,256]{3,2,1,0:T(8,128)}), f32[256,2,8,256]{3,2,1,0:T(8,128)}, u32[]{:S(2)}, u32[]{:S(2)}) %all-to-all-start.1) | async-done | bytes 4194336 | tf_op jit(solution)/shard_map/all_to_all | solution.py:225
  199.5 9.5 %shard_map.64 = f32[2048,128]{1,0:T(8,128)} custom-call(f32[32,8,2,8,256]{4,3,2,1,0:T(8,128)} %bitcast.78, f32[32,8,2,8,256]{4,3,2,1,0:T(8,128)} %bitcast.11.great_hbm, bf16[128,256]{1,0:T(8,128)(2,1)} %constant.14.clone.there, bf16[64,384]{1,0:T(8,128)(2,1)} %constant.15.clone.back), custom_call_target="tpu_custom_call" | custom-call | flops 4000000000 | bytes 9500000 | tf_op jit(solution)/shard_map/pallas_call | solution.py:127
  209.1 53.7 %all_to_all.15 = f32[64,2,2,8,128]{4,3,2,1,0:T(8,128)S(1)} all-to-all(f32[64,2,2,8,128]{4,3,2,1,0:T(8,128)} %bitcast.79), channel_id=1, replica_groups=mesh['xz'=16,'core'=2,'y'=4,'zl'=2] {'xz','core','zl'}, dimensions={0} | all-to-all | bytes 2097152 | tf_op jit(solution)/shard_map/all_to_all | solution.py:229
  262.8 0.0 copy-start
  262.8 0.1 select_bitcast_fusion.1
  262.9 2.4 collective-permute-start.4
  265.3 3.5 %collective-permute-start.3 = (f32[32,2,2,8,128]{4,3,2,1,0:T(8,128)S(1)}, f32[32,2,2,8,128]{4,3,2,1,0:T(8,128)S(1)}, u32[]{:S(2)}, u32[]{:S(2)}) collective-permute-start(f32[32,2,2,8,128]{4,3,2,1,0:T(8,128)S(1)} %get-tuple-element.28.far.near), channel_id=1, source_target_pairs={{0,2},{2,4},{3,1},{4,6},{5,3},{7,5},{8,10},{10,12},{11,9},{12,14},... | collective-permute-start | bytes 1572872 | tf_op jit(solution)/shard_map/ppermute | solution.py:247
  268.8 2.4 collective-permute-start.6
  271.2 1.6 collective-permute-done.4.outer
  272.8 1.2 shard_map.66
  274.0 0.7 collective-permute-start.5
  274.7 3.4 %collective-permute-done.6.outer = f32[32,2,8,128]{3,2,1,0:T(8,128)S(1)} collective-permute-done((f32[32,2,8,128]{3,2,1,0:T(8,128)S(1)}, f32[32,2,8,128]{3,2,1,0:T(8,128)S(1)}, u32[]{:S(2)}, u32[]{:S(2)}) %collective-permute-start.6) | collective-permute-done | bytes 262176 | tf_op jit(solution)/shard_map/ppermute | solution.py:246
  278.1 1.2 shard_map.67
  279.3 0.7 collective-permute-start.7
  280.0 0.2 collective-permute-done.3.outer
  280.2 0.0 copy-done
  280.2 1.6 shard_map.65
  281.8 0.0 collective-permute-done.5
  281.8 4.5 %collective-permute-done.7 = f32[256,256]{1,0:T(8,128)S(1)} collective-permute-done((f32[256,256]{1,0:T(8,128)S(1)}, f32[256,256]{1,0:T(8,128)S(1)}, u32[]{:S(2)}, u32[]{:S(2)}) %collective-permute-start.7) | collective-permute-done | bytes 262176 | tf_op jit(solution)/shard_map/ppermute | solution.py:255
  286.2 0.1 select_bitcast_fusion.5
  286.3 1.0 pad_maximum_fusion
  (3 shorter events, 0.1 us)
Async XLA Ops:
  1.1 8.3 %collective-permute-start = (f32[256,256]{1,0:T(8,128)S(1)}, f32[256,256]{1,0:T(8,128)S(1)}, u32[]{:S(2)}, u32[]{:S(2)}) collective-permute-start(f32[256,256]{1,0:T(8,128)S(1)} %bitcast_select_fusion.6), channel_id=1, source_target_pairs={{0,1},{1,0},{2,3},{3,2},{4,5},{5,4},{6,7},{7,6},{8,9},{9,8},{10,11... | collective-permute-start | bytes 786440 | tf_op jit(solution)/shard_map/ppermute | solution.py:207
  7.9 14.4 %copy-start.1 = (f32[1,256,256]{2,1,0:T(8,128)S(1)}, f32[1,256,256]{2,1,0:T(8,128)}, u32[]{:S(2)}) copy-start(f32[1,256,256]{2,1,0:T(8,128)} %param.9) | copy-start | bytes 786436
  9.4 104.2 %all-to-all-start = ((f32[32,2,8,8,256]{4,3,2,1,0:T(8,128)}), f32[32,2,8,8,256]{4,3,2,1,0:T(8,128)}, u32[]{:S(2)}, u32[]{:S(2)}) async-start(f32[32,2,8,8,256]{4,3,2,1,0:T(8,128)} %copy_bitcast_fusion.1), calls=%async_computation | async-start | bytes 8388608 | tf_op jit(solution)/shard_map/all_to_all | solution.py:210
  20.7 1.6 collective-permute-start.1
  22.3 10.3 %collective-permute-start.2 = (f32[256,256]{1,0:T(8,128)S(1)}, f32[256,256]{1,0:T(8,128)S(1)}, u32[]{:S(2)}, u32[]{:S(2)}) collective-permute-start(f32[256,256]{1,0:T(8,128)S(1)} %get-tuple-element.33), channel_id=1, source_target_pairs={{0,2},{2,4},{4,6},{1,3},{3,5},{5,7},{8,10},{10,12},{12,14},{9,11},... | collective-permute-start | bytes 786440 | tf_op jit(solution)/shard_map/ppermute | solution.py:216
  113.6 85.9 %all-to-all-start.1 = ((f32[256,2,8,256]{3,2,1,0:T(8,128)}), f32[256,2,8,256]{3,2,1,0:T(8,128)}, u32[]{:S(2)}, u32[]{:S(2)}) async-start(f32[256,2,8,256]{3,2,1,0:T(8,128)} %bitcast.76), calls=%async_computation.1 | async-start | bytes 8388608 | tf_op jit(solution)/shard_map/all_to_all | solution.py:225
  262.8 17.4 %copy-start = (f32[1,256,256]{2,1,0:T(8,128)S(1)}, f32[1,256,256]{2,1,0:T(8,128)}, u32[]{:S(2)}) copy-start(f32[1,256,256]{2,1,0:T(8,128)} %param.8) | copy-start | bytes 786436
  262.9 9.9 %collective-permute-start.4 = (f32[32,2,8,128]{3,2,1,0:T(8,128)S(1)}, f32[32,2,8,128]{3,2,1,0:T(8,128)S(1)}, u32[]{:S(2)}, u32[]{:S(2)}) collective-permute-start(f32[32,2,8,128]{3,2,1,0:T(8,128)S(1)} %get-tuple-element.37), channel_id=1, source_target_pairs={{1,3},{2,0},{3,5},{4,2},{5,7},{6,4},{9,11},{10,8},{11,13},{12,10},... | collective-permute-start | bytes 786440 | tf_op jit(solution)/shard_map/ppermute | solution.py:246
  265.3 14.9 %collective-permute-start.3 = (f32[32,2,2,8,128]{4,3,2,1,0:T(8,128)S(1)}, f32[32,2,2,8,128]{4,3,2,1,0:T(8,128)S(1)}, u32[]{:S(2)}, u32[]{:S(2)}) collective-permute-start(f32[32,2,2,8,128]{4,3,2,1,0:T(8,128)S(1)} %get-tuple-element.28.far.near), channel_id=1, source_target_pairs={{0,2},{2,4},{3,1},{4,6},{5,3},{7,5},{8,10},{10,12},{11,9},{12,14},... | collective-permute-start | bytes 1572872 | tf_op jit(solution)/shard_map/ppermute | solution.py:247
  268.8 9.3 %collective-permute-start.6 = (f32[32,2,8,128]{3,2,1,0:T(8,128)S(1)}, f32[32,2,8,128]{3,2,1,0:T(8,128)S(1)}, u32[]{:S(2)}, u32[]{:S(2)}) collective-permute-start(f32[32,2,8,128]{3,2,1,0:T(8,128)S(1)} %get-tuple-element.38), channel_id=1, source_target_pairs={{1,3},{2,0},{3,5},{4,2},{5,7},{6,4},{9,11},{10,8},{11,13},{12,10},... | collective-permute-start | bytes 786440 | tf_op jit(solution)/shard_map/ppermute | solution.py:246
  274.0 7.8 %collective-permute-start.5 = (f32[256,256]{1,0:T(8,128)S(1)}, f32[256,256]{1,0:T(8,128)S(1)}, u32[]{:S(2)}, u32[]{:S(2)}) collective-permute-start(f32[256,256]{1,0:T(8,128)S(1)} %shard_map.66), channel_id=1, source_target_pairs={{0,1},{1,0},{2,3},{3,2},{4,5},{5,4},{6,7},{7,6},{8,9},{9,8},{10,11... | collective-permute-start | bytes 786440 | tf_op jit(solution)/shard_map/ppermute | solution.py:255
  279.3 6.9 %collective-permute-start.7 = (f32[256,256]{1,0:T(8,128)S(1)}, f32[256,256]{1,0:T(8,128)S(1)}, u32[]{:S(2)}, u32[]{:S(2)}) collective-permute-start(f32[256,256]{1,0:T(8,128)S(1)} %shard_map.67), channel_id=1, source_target_pairs={{0,1},{1,0},{2,3},{3,2},{4,5},{5,4},{6,7},{7,6},{8,9},{9,8},{10,11... | collective-permute-start | bytes 786440 | tf_op jit(solution)/shard_map/ppermute | solution.py:255

commit v4 on v3

--- a/solution.py
+++ b/solution.py
@@ -94,16 +94,24 @@
     return out[:, : re.shape[1]], out[:, re.shape[1] :]
 
 
-def polar_kernel(less_hbm, great_hbm, there, back, out_ref, held, sems):
+def polar_kernel(less_hbm, great_hbm, there_hbm, back_hbm, out_ref, held, there, back, sems):
     rows = held.shape[1]
 
     def copy(which, i):
         source = (less_hbm, great_hbm)[which]
         return pltpu.make_async_copy(source.at[:, i], held.at[which, i], sems.at[which, i])
 
+    fixed = (
+        pltpu.make_async_copy(there_hbm, there, sems.at[0, rows]),
+        pltpu.make_async_copy(back_hbm, back, sems.at[1, rows]),
+    )
+    for table in fixed:
+        table.start()
     for i in range(rows):
         copy(0, i).start()
         copy(1, i).start()
+    for table in fixed:
+        table.wait()
 
     def row(i, carry):
         copy(0, i).wait()
@@ -126,12 +134,14 @@
     vmem = pl.BlockSpec(memory_space=pltpu.VMEM)
     out = pl.pallas_call(
         polar_kernel,
-        in_specs=[hbm, hbm, vmem, vmem],
+        in_specs=[hbm] * 4,
         out_specs=vmem,
         out_shape=jax.ShapeDtypeStruct((NW * 2 * rows * columns // LANES, LANES), jnp.float32),
         scratch_shapes=[
             pltpu.VMEM((2, rows, sources, 2, local, columns), jnp.float32),
-            pltpu.SemaphoreType.DMA((2, rows)),
+            pltpu.VMEM(there.shape, there.dtype),
+            pltpu.VMEM(back.shape, back.dtype),
+            pltpu.SemaphoreType.DMA((2, rows + 1)),
         ],
         compiler_params=pltpu.CompilerParams(vmem_limit_bytes=57 * 1024 * 1024),
         cost_estimate=pl.CostEstimate(
@@ -206,8 +216,8 @@
     v, u = v_diag[0], v_upper[0]
     theirs = lax.ppermute(plain(jnp.where(first_core, v, u)), "zl", SWAP)
     less_send = g_lesser.reshape(2, -1, devices, rows, size).transpose(2, 0, 1, 3, 4)
-    less_send, theirs = lax.optimization_barrier((plain(less_send), theirs))
-    less = plain(lax.all_to_all(plain(less_send), ENERGY, split_axis=0, concat_axis=0, tiled=True))
+    less = lax.all_to_all(lax.optimization_barrier(plain(less_send)), ENERGY, split_axis=0, concat_axis=0, tiled=True)
+    less = plain(less)
 
     other = lax.ppermute(theirs, "core", SWAP)
     v_pair = jnp.where(first_core, theirs, other)

time: 288 us -> 300 us (1.042)
  waiting for transfers between devices: 166 us -> 197 us
  blocking collectives: 53.7 us -> 37.4 us
    ppermute x1, waiting for transfers between devices: 1.52 us -> 96.5 us  [local(): theirs = lax.ppermute(plain(jnp.where(first_core, v, u)), 'zl', SWAP)]
    all_to_all x1, waiting for transfers between devices: 80.5 us -> 0.01 us  [local(): lax.all_to_all(lax.optimization_barrier(plain(less_send)), ENERGY, split_...]
    all_to_all x1, blocking collectives: 53.7 us -> 37.4 us  [local(): lax.all_to_all(plain(polar), ENERGY + ('zl',), split_axis=0, concat_axis=...]
    all_to_all x1, waiting for transfers between devices: 72.2 us -> 87.6 us  [local(): lax.all_to_all(great_send, ENERGY, split_axis=0, concat_axis=0, tiled=True)]
  transfers between devices with their start and end apart: 10 -> 10, of which waited for: 9 -> 7; matrix products, arithmetic and copies ran while one was open for 6% -> 4% of each run, Pallas kernels for 1% -> 1%
where the time goes in v4:
time: 300 us
  waiting for transfers between devices  197 us (66%)
  blocking collectives  37.4 us (12%)
  starting transfers between devices  34.6 us (12%)
  local copies, waits for them, and re-layouts  16.7 us (6%)
  Pallas kernels  12.8 us (4%)
    ppermute x1, waiting for transfers between devices, local(): theirs = lax.ppermute(plain(jnp.where(first_core, v, u)), 'zl', SWAP)  96.5 us
    all_to_all x1, waiting for transfers between devices, local(): lax.all_to_all(great_send, ENERGY, split_axis=0, concat_axis=0, tiled=True)  87.6 us
    all_to_all x1, blocking collectives, local(): lax.all_to_all(plain(polar), ENERGY + ('zl',), split_axis=0, concat_axis=...  37.4 us
    all_to_all x1, starting transfers between devices, local(): lax.all_to_all(lax.optimization_barrier(plain(less_send)), ENERGY, split_...  11.6 us
    all_to_all x1, starting transfers between devices, local(): lax.all_to_all(great_send, ENERGY, split_axis=0, concat_axis=0, tiled=True)  9.29 us
    pallas_call x1, Pallas kernels, polar_of(): pl.pallas_call(polar_kernel, in_specs=[hbm] * 4, out_specs=vmem, out_shap...  8.76 us
  transfers between devices with their start and end apart: 10, of which 7 were waited for; matrix products, arithmetic and copies ran while one was open for 4% of the time, Pallas kernels for 1%

profile of v4, /device:TPU:8, one launch (start us, length us, event | category | flops | bytes accessed | tf_op | source)
XLA Modules:
  0.0 299.8 jit_solution(6647489287849810230)
XLA Ops:
  0.0 4.8 %copy_bitcast_fusion.1 = f32[32,2,8,8,256]{4,3,2,1,0:T(8,128)} fusion(f32[2,8,1,256,256]{4,3,2,1,0:T(8,128)} %param.6), kind=kLoop, calls=%fused_computation.1 | loop fusion | bytes 8388608 | tf_op jit(solution)/shard_map/transpose | solution.py:218
  4.8 0.0 copy-start
  4.8 0.0 copy-start.1
  4.8 11.6 %all-to-all-start = ((f32[32,2,8,8,256]{4,3,2,1,0:T(8,128)}), f32[32,2,8,8,256]{4,3,2,1,0:T(8,128)}, u32[]{:S(2)}, u32[]{:S(2)}) async-start(f32[32,2,8,8,256]{4,3,2,1,0:T(8,128)} %copy_bitcast_fusion.1), calls=%async_computation | async-start | bytes 8388608 | tf_op jit(solution)/shard_map/all_to_all | solution.py:219
  16.4 0.0 copy-done
  16.4 0.0 copy-done.1
  16.4 1.1 collective-permute-start
  17.5 96.5 %collective-permute-done = f32[256,256]{1,0:T(8,128)S(1)} collective-permute-done((f32[256,256]{1,0:T(8,128)S(1)}, f32[256,256]{1,0:T(8,128)S(1)}, u32[]{:S(2)}, u32[]{:S(2)}) %collective-permute-start) | collective-permute-done | bytes 262176 | tf_op jit(solution)/shard_map/ppermute | solution.py:217
  114.0 0.0 collective-permute-start.1
  114.0 1.5 collective-permute-done.1
  115.6 0.1 bitcast_select_fusion.4
  115.6 3.5 %collective-permute-start.2 = (f32[256,256]{1,0:T(8,128)S(1)}, f32[256,256]{1,0:T(8,128)S(1)}, u32[]{:S(2)}, u32[]{:S(2)}) collective-permute-start(f32[256,256]{1,0:T(8,128)S(1)} %get-tuple-element.29), channel_id=1, source_target_pairs={{0,2},{2,4},{4,6},{1,3},{3,5},{5,7},{8,10},{10,12},{12,14},{9,11},... | collective-permute-start | bytes 786440 | tf_op jit(solution)/shard_map/ppermute | solution.py:226
  119.1 5.5 %copy.28 = f32[2,8,1,256,256]{3,1,0,4,2:T(8,128)} copy(f32[2,8,1,256,256]{4,3,2,1,0:T(8,128)} %param.7) | data formatting | bytes 8388608 | tf_op args[1]
  124.7 0.1 copy.29
  124.8 1.0 collective-permute-done.2
  125.9 0.1 copy.30
  126.0 0.1 copy.31.a_t
  126.2 0.1 copy.32.a_t
  126.3 0.0 all-to-all-done
  126.3 9.3 %all-to-all-start.1 = ((f32[256,2,8,256]{3,2,1,0:T(8,128)}), f32[256,2,8,256]{3,2,1,0:T(8,128)}, u32[]{:S(2)}, u32[]{:S(2)}) async-start(f32[256,2,8,256]{3,2,1,0:T(8,128)} %bitcast.76), calls=%async_computation.1 | async-start | bytes 8388608 | tf_op jit(solution)/shard_map/all_to_all | solution.py:235
  135.6 5.8 %copy.43 = f32[32,2,8,8,256]{4,2,1,3,0:T(8,128)} copy(f32[32,2,8,8,256]{4,3,2,1,0:T(8,128)} %all-to-all-done) | data formatting | bytes 8388608 | tf_op jit(solution)/shard_map/layout_constraint | solution.py:204
  141.5 87.6 %all-to-all-done.1 = f32[256,2,8,256]{3,2,1,0:T(8,128)} async-done(((f32[256,2,8,256]{3,2,1,0:T(8,128)}), f32[256,2,8,256]{3,2,1,0:T(8,128)}, u32[]{:S(2)}, u32[]{:S(2)}) %all-to-all-start.1) | async-done | bytes 4194336 | tf_op jit(solution)/shard_map/all_to_all | solution.py:235
  229.1 8.8 %shard_map.64 = f32[2048,128]{1,0:T(8,128)} custom-call(f32[32,8,2,8,256]{4,3,2,1,0:T(8,128)} %bitcast.78, f32[32,8,2,8,256]{4,3,2,1,0:T(8,128)} %bitcast.11.great_hbm, bf16[128,256]{1,0:T(8,128)(2,1)} %constant.14.clone.there_hbm, bf16[64,384]{1,0:T(8,128)(2,1)} %constant.15.clone.back_hbm), custom_call_target="tpu_custom_call" | custom-call | flops 4000000000 | bytes 9500000 | tf_op jit(solution)/shard_map/pallas_call | solution.py:135
  237.9 37.4 %all_to_all.15 = f32[64,2,2,8,128]{4,3,2,1,0:T(8,128)S(1)} all-to-all(f32[64,2,2,8,128]{4,3,2,1,0:T(8,128)} %bitcast.79), channel_id=1, replica_groups=mesh['xz'=16,'core'=2,'y'=4,'zl'=2] {'xz','core','zl'}, dimensions={0} | all-to-all | bytes 2097152 | tf_op jit(solution)/shard_map/all_to_all | solution.py:239
  275.2 0.1 select_bitcast_fusion.1
  275.4 1.9 collective-permute-start.4
  277.3 3.9 %collective-permute-start.3 = (f32[32,2,2,8,128]{4,3,2,1,0:T(8,128)S(1)}, f32[32,2,2,8,128]{4,3,2,1,0:T(8,128)S(1)}, u32[]{:S(2)}, u32[]{:S(2)}) collective-permute-start(f32[32,2,2,8,128]{4,3,2,1,0:T(8,128)S(1)} %get-tuple-element.24.far.near), channel_id=1, source_target_pairs={{0,2},{2,4},{3,1},{4,6},{5,3},{7,5},{8,10},{10,12},{11,9},{12,14},... | collective-permute-start | bytes 1572872 | tf_op jit(solution)/shard_map/ppermute | solution.py:257
  281.2 1.9 collective-permute-start.6
  283.2 2.1 collective-permute-done.4.outer
  285.3 1.2 shard_map.66
  286.5 0.7 collective-permute-start.5
  287.2 3.4 %collective-permute-done.6.outer = f32[32,2,8,128]{3,2,1,0:T(8,128)S(1)} collective-permute-done((f32[32,2,8,128]{3,2,1,0:T(8,128)S(1)}, f32[32,2,8,128]{3,2,1,0:T(8,128)S(1)}, u32[]{:S(2)}, u32[]{:S(2)}) %collective-permute-start.6) | collective-permute-done | bytes 262176 | tf_op jit(solution)/shard_map/ppermute | solution.py:256
  290.6 1.2 shard_map.67
  291.8 0.7 collective-permute-start.7
  292.5 0.0 collective-permute-done.3.outer
  292.5 1.6 shard_map.65
  294.1 0.0 collective-permute-done.5
  294.1 4.6 %collective-permute-done.7 = f32[256,256]{1,0:T(8,128)S(1)} collective-permute-done((f32[256,256]{1,0:T(8,128)S(1)}, f32[256,256]{1,0:T(8,128)S(1)}, u32[]{:S(2)}, u32[]{:S(2)}) %collective-permute-start.7) | collective-permute-done | bytes 262176 | tf_op jit(solution)/shard_map/ppermute | solution.py:265
  298.7 0.1 select_bitcast_fusion.5
  298.8 1.0 pad_maximum_fusion
  (4 shorter events, 0.1 us)
Async XLA Ops:
  4.8 11.6 %copy-start = (f32[1,256,256]{2,1,0:T(8,128)S(1)}, f32[1,256,256]{2,1,0:T(8,128)}, u32[]{:S(2)}) copy-start(f32[1,256,256]{2,1,0:T(8,128)} %param.8) | copy-start | bytes 786436
  4.8 11.6 %copy-start.1 = (f32[1,256,256]{2,1,0:T(8,128)S(1)}, f32[1,256,256]{2,1,0:T(8,128)}, u32[]{:S(2)}) copy-start(f32[1,256,256]{2,1,0:T(8,128)} %param.9) | copy-start | bytes 786436
  4.8 121.5 %all-to-all-start = ((f32[32,2,8,8,256]{4,3,2,1,0:T(8,128)}), f32[32,2,8,8,256]{4,3,2,1,0:T(8,128)}, u32[]{:S(2)}, u32[]{:S(2)}) async-start(f32[32,2,8,8,256]{4,3,2,1,0:T(8,128)} %copy_bitcast_fusion.1), calls=%async_computation | async-start | bytes 8388608 | tf_op jit(solution)/shard_map/all_to_all | solution.py:219
  16.4 97.6 %collective-permute-start = (f32[256,256]{1,0:T(8,128)S(1)}, f32[256,256]{1,0:T(8,128)S(1)}, u32[]{:S(2)}, u32[]{:S(2)}) collective-permute-start(f32[256,256]{1,0:T(8,128)S(1)} %bitcast_select_fusion.6), channel_id=1, source_target_pairs={{0,1},{1,0},{2,3},{3,2},{4,5},{5,4},{6,7},{7,6},{8,9},{9,8},{10,11... | collective-permute-start | bytes 786440 | tf_op jit(solution)/shard_map/ppermute | solution.py:217
  114.0 1.5 collective-permute-start.1
  115.6 10.2 %collective-permute-start.2 = (f32[256,256]{1,0:T(8,128)S(1)}, f32[256,256]{1,0:T(8,128)S(1)}, u32[]{:S(2)}, u32[]{:S(2)}) collective-permute-start(f32[256,256]{1,0:T(8,128)S(1)} %get-tuple-element.29), channel_id=1, source_target_pairs={{0,2},{2,4},{4,6},{1,3},{3,5},{5,7},{8,10},{10,12},{12,14},{9,11},... | collective-permute-start | bytes 786440 | tf_op jit(solution)/shard_map/ppermute | solution.py:226
  126.3 102.8 %all-to-all-start.1 = ((f32[256,2,8,256]{3,2,1,0:T(8,128)}), f32[256,2,8,256]{3,2,1,0:T(8,128)}, u32[]{:S(2)}, u32[]{:S(2)}) async-start(f32[256,2,8,256]{3,2,1,0:T(8,128)} %bitcast.76), calls=%async_computation.1 | async-start | bytes 8388608 | tf_op jit(solution)/shard_map/all_to_all | solution.py:235
  275.4 9.9 %collective-permute-start.4 = (f32[32,2,8,128]{3,2,1,0:T(8,128)S(1)}, f32[32,2,8,128]{3,2,1,0:T(8,128)S(1)}, u32[]{:S(2)}, u32[]{:S(2)}) collective-permute-start(f32[32,2,8,128]{3,2,1,0:T(8,128)S(1)} %get-tuple-element.33), channel_id=1, source_target_pairs={{1,3},{2,0},{3,5},{4,2},{5,7},{6,4},{9,11},{10,8},{11,13},{12,10},... | collective-permute-start | bytes 786440 | tf_op jit(solution)/shard_map/ppermute | solution.py:256
  277.3 15.2 %collective-permute-start.3 = (f32[32,2,2,8,128]{4,3,2,1,0:T(8,128)S(1)}, f32[32,2,2,8,128]{4,3,2,1,0:T(8,128)S(1)}, u32[]{:S(2)}, u32[]{:S(2)}) collective-permute-start(f32[32,2,2,8,128]{4,3,2,1,0:T(8,128)S(1)} %get-tuple-element.24.far.near), channel_id=1, source_target_pairs={{0,2},{2,4},{3,1},{4,6},{5,3},{7,5},{8,10},{10,12},{11,9},{12,14},... | collective-permute-start | bytes 1572872 | tf_op jit(solution)/shard_map/ppermute | solution.py:257
  281.2 9.3 %collective-permute-start.6 = (f32[32,2,8,128]{3,2,1,0:T(8,128)S(1)}, f32[32,2,8,128]{3,2,1,0:T(8,128)S(1)}, u32[]{:S(2)}, u32[]{:S(2)}) collective-permute-start(f32[32,2,8,128]{3,2,1,0:T(8,128)S(1)} %get-tuple-element.34), channel_id=1, source_target_pairs={{1,3},{2,0},{3,5},{4,2},{5,7},{6,4},{9,11},{10,8},{11,13},{12,10},... | collective-permute-start | bytes 786440 | tf_op jit(solution)/shard_map/ppermute | solution.py:256
  286.5 7.6 %collective-permute-start.5 = (f32[256,256]{1,0:T(8,128)S(1)}, f32[256,256]{1,0:T(8,128)S(1)}, u32[]{:S(2)}, u32[]{:S(2)}) collective-permute-start(f32[256,256]{1,0:T(8,128)S(1)} %shard_map.66), channel_id=1, source_target_pairs={{0,1},{1,0},{2,3},{3,2},{4,5},{5,4},{6,7},{7,6},{8,9},{9,8},{10,11... | collective-permute-start | bytes 786440 | tf_op jit(solution)/shard_map/ppermute | solution.py:265
  291.8 6.9 %collective-permute-start.7 = (f32[256,256]{1,0:T(8,128)S(1)}, f32[256,256]{1,0:T(8,128)S(1)}, u32[]{:S(2)}, u32[]{:S(2)}) collective-permute-start(f32[256,256]{1,0:T(8,128)S(1)} %shard_map.67), channel_id=1, source_target_pairs={{0,1},{1,0},{2,3},{3,2},{4,5},{5,4},{6,7},{7,6},{8,9},{9,8},{10,11... | collective-permute-start | bytes 786440 | tf_op jit(solution)/shard_map/ppermute | solution.py:265

commit v5 on v4

--- a/solution.py
+++ b/solution.py
@@ -173,9 +173,16 @@
     return [x + y + z for x, y, z in zip(*terms)]
 
 
-def send_kernel(c, near, far, outer, v, w, w_t, a, a_t, out_ref):
-    blocks = ([block_of(near, c)], [block_of(far, c)], [block_of(outer)])
-    (out_ref[...],) = screen(*blocks, v[...], w[...], w_t[...], a[...], a_t[...])
+def pair_kernel(near, far, v, w, w_t, out_ref):
+    blocks = [[block_of(ref, c) for c in range(2)] for ref in (near, far)]
+    terms = sandwich(v[...], blocks[0], v[...]), sandwich(w[...], blocks[1], w_t[...])
+    for c, (x, y) in enumerate(zip(*terms)):
+        out_ref[c] = x + y
+
+
+def send_kernel(c, part, outer, a, a_t, out_ref):
+    (term,) = sandwich(a[...], [block_of(outer)], a_t[...])
+    out_ref[...] = part[c] + term
 
 
 def own_kernel(near, far, outer, v, w, w_t, a, a_t, out_ref):
@@ -256,11 +263,12 @@
         for_send.append(lax.ppermute(plain(far[:, c]), SPACE, toward))
     for_own = lax.ppermute(near, SPACE, away)
 
+    part = on_core(pair_kernel, (2, size, size), 800_000_000, near, far, v_pair, w, w_t)
     got = []
     for c in range(2):
         ready = on_core(
-            functools.partial(send_kernel, c), (size, size), 600_000_000,
-            near, far, for_send[c], v_pair, w, w_t, sends, sends_t,
+            functools.partial(send_kernel, c), (size, size), 200_000_000,
+            part, for_send[c], sends, sends_t,
         )
         got.append(plain(lax.ppermute(plain(ready), "zl", SWAP)))
     kept = on_core(

time: 300 us -> 304 us (1.013)
  waiting for transfers between devices: 197 us -> 202 us
    ppermute x2, waiting for transfers between devices: 5.48 us -> 8.79 us  [local(): for_send.append(lax.ppermute(plain(far[:, c]), SPACE, toward))]
  transfers between devices with their start and end apart: 10 -> 10, of which waited for: 7 -> 8; matrix products, arithmetic and copies ran while one was open for 4% -> 4% of each run, Pallas kernels for 1% -> 1%
where the time goes in v5:
time: 304 us
  waiting for transfers between devices  202 us (66%)
  blocking collectives  37.4 us (12%)
  starting transfers between devices  33.4 us (11%)
  local copies, waits for them, and re-layouts  16.7 us (5%)
  Pallas kernels  12.6 us (4%)
    ppermute x1, waiting for transfers between devices, local(): theirs = lax.ppermute(plain(jnp.where(first_core, v, u)), 'zl', SWAP)  96.5 us
    all_to_all x1, waiting for transfers between devices, local(): lax.all_to_all(great_send, ENERGY, split_axis=0, concat_axis=0, tiled=True)  87.6 us
    all_to_all x1, blocking collectives, local(): lax.all_to_all(plain(polar), ENERGY + ('zl',), split_axis=0, concat_axis=...  37.4 us
    all_to_all x1, starting transfers between devices, local(): lax.all_to_all(lax.optimization_barrier(plain(less_send)), ENERGY, split_...  11.6 us
    all_to_all x1, starting transfers between devices, local(): lax.all_to_all(great_send, ENERGY, split_axis=0, concat_axis=0, tiled=True)  9.29 us
    ppermute x2, waiting for transfers between devices, local(): for_send.append(lax.ppermute(plain(far[:, c]), SPACE, toward))  8.79 us
    pallas_call x1, Pallas kernels, polar_of(): pl.pallas_call(polar_kernel, in_specs=[hbm] * 4, out_specs=vmem, out_shap...  8.76 us
    ppermute x2, waiting for transfers between devices, local(): got.append(plain(lax.ppermute(plain(ready), 'zl', SWAP)))  6.56 us
  transfers between devices with their start and end apart: 10, of which 8 were waited for; matrix products, arithmetic and copies ran while one was open for 4% of the time, Pallas kernels for 1%

profile of v5, /device:TPU:8, one launch (start us, length us, event | category | flops | bytes accessed | tf_op | source)
XLA Modules:
  0.0 303.8 jit_solution(17590429920083058087)
XLA Ops:
  0.0 4.8 %copy_bitcast_fusion.1 = f32[32,2,8,8,256]{4,3,2,1,0:T(8,128)} fusion(f32[2,8,1,256,256]{4,3,2,1,0:T(8,128)} %param.6), kind=kLoop, calls=%fused_computation.1 | loop fusion | bytes 8388608 | tf_op jit(solution)/shard_map/transpose | solution.py:225
  4.8 0.0 copy-start
  4.8 0.0 copy-start.1
  4.8 11.6 %all-to-all-start = ((f32[32,2,8,8,256]{4,3,2,1,0:T(8,128)}), f32[32,2,8,8,256]{4,3,2,1,0:T(8,128)}, u32[]{:S(2)}, u32[]{:S(2)}) async-start(f32[32,2,8,8,256]{4,3,2,1,0:T(8,128)} %copy_bitcast_fusion.1), calls=%async_computation | async-start | bytes 8388608 | tf_op jit(solution)/shard_map/all_to_all | solution.py:226
  16.4 0.0 copy-done
  16.4 0.0 copy-done.1
  16.4 1.1 collective-permute-start
  17.5 96.5 %collective-permute-done = f32[256,256]{1,0:T(8,128)S(1)} collective-permute-done((f32[256,256]{1,0:T(8,128)S(1)}, f32[256,256]{1,0:T(8,128)S(1)}, u32[]{:S(2)}, u32[]{:S(2)}) %collective-permute-start) | collective-permute-done | bytes 262176 | tf_op jit(solution)/shard_map/ppermute | solution.py:224
  114.0 0.0 collective-permute-start.1
  114.0 1.5 collective-permute-done.1
  115.6 0.1 bitcast_select_fusion.4
  115.6 3.5 %collective-permute-start.2 = (f32[256,256]{1,0:T(8,128)S(1)}, f32[256,256]{1,0:T(8,128)S(1)}, u32[]{:S(2)}, u32[]{:S(2)}) collective-permute-start(f32[256,256]{1,0:T(8,128)S(1)} %get-tuple-element.29), channel_id=1, source_target_pairs={{0,2},{2,4},{4,6},{1,3},{3,5},{5,7},{8,10},{10,12},{12,14},{9,11},... | collective-permute-start | bytes 786440 | tf_op jit(solution)/shard_map/ppermute | solution.py:233
  119.1 5.5 %copy.28 = f32[2,8,1,256,256]{3,1,0,4,2:T(8,128)} copy(f32[2,8,1,256,256]{4,3,2,1,0:T(8,128)} %param.7) | data formatting | bytes 8388608 | tf_op args[1]
  124.7 0.1 copy.29
  124.8 1.0 collective-permute-done.2
  125.9 0.1 copy.30
  126.0 0.1 copy.31.a_t
  126.2 0.1 copy.32.a_t
  126.3 0.0 all-to-all-done
  126.3 9.3 %all-to-all-start.1 = ((f32[256,2,8,256]{3,2,1,0:T(8,128)}), f32[256,2,8,256]{3,2,1,0:T(8,128)}, u32[]{:S(2)}, u32[]{:S(2)}) async-start(f32[256,2,8,256]{3,2,1,0:T(8,128)} %bitcast.76), calls=%async_computation.1 | async-start | bytes 8388608 | tf_op jit(solution)/shard_map/all_to_all | solution.py:242
  135.6 5.8 %copy.43 = f32[32,2,8,8,256]{4,2,1,3,0:T(8,128)} copy(f32[32,2,8,8,256]{4,3,2,1,0:T(8,128)} %all-to-all-done) | data formatting | bytes 8388608 | tf_op jit(solution)/shard_map/layout_constraint | solution.py:211
  141.5 87.6 %all-to-all-done.1 = f32[256,2,8,256]{3,2,1,0:T(8,128)} async-done(((f32[256,2,8,256]{3,2,1,0:T(8,128)}), f32[256,2,8,256]{3,2,1,0:T(8,128)}, u32[]{:S(2)}, u32[]{:S(2)}) %all-to-all-start.1) | async-done | bytes 4194336 | tf_op jit(solution)/shard_map/all_to_all | solution.py:242
  229.1 8.8 %shard_map.64 = f32[2048,128]{1,0:T(8,128)} custom-call(f32[32,8,2,8,256]{4,3,2,1,0:T(8,128)} %bitcast.78, f32[32,8,2,8,256]{4,3,2,1,0:T(8,128)} %bitcast.11.great_hbm, bf16[128,256]{1,0:T(8,128)(2,1)} %constant.14.clone.there_hbm, bf16[64,384]{1,0:T(8,128)(2,1)} %constant.15.clone.back_hbm), custom_call_target="tpu_custom_call" | custom-call | flops 4000000000 | bytes 9500000 | tf_op jit(solution)/shard_map/pallas_call | solution.py:135
  237.9 37.4 %all_to_all.15 = f32[64,2,2,8,128]{4,3,2,1,0:T(8,128)S(1)} all-to-all(f32[64,2,2,8,128]{4,3,2,1,0:T(8,128)} %bitcast.79), channel_id=1, replica_groups=mesh['xz'=16,'core'=2,'y'=4,'zl'=2] {'xz','core','zl'}, dimensions={0} | all-to-all | bytes 2097152 | tf_op jit(solution)/shard_map/all_to_all | solution.py:246
  275.2 0.1 select_bitcast_fusion.1
  275.3 3.5 %collective-permute-start.3 = (f32[32,2,2,8,128]{4,3,2,1,0:T(8,128)S(1)}, f32[32,2,2,8,128]{4,3,2,1,0:T(8,128)S(1)}, u32[]{:S(2)}, u32[]{:S(2)}) collective-permute-start(f32[32,2,2,8,128]{4,3,2,1,0:T(8,128)S(1)} %get-tuple-element.24.far.near), channel_id=1, source_target_pairs={{0,2},{2,4},{3,1},{4,6},{5,3},{7,5},{8,10},{10,12},{11,9},{12,14},... | collective-permute-start | bytes 1572872 | tf_op jit(solution)/shard_map/ppermute | solution.py:264
  278.9 2.4 collective-permute-start.4
  281.3 1.9 collective-permute-start.6
  283.2 1.1 shard_map.66.part
  284.3 5.7 %collective-permute-done.4.outer = f32[32,2,8,128]{3,2,1,0:T(8,128)S(1)} collective-permute-done((f32[32,2,8,128]{3,2,1,0:T(8,128)S(1)}, f32[32,2,8,128]{3,2,1,0:T(8,128)S(1)}, u32[]{:S(2)}, u32[]{:S(2)}) %collective-permute-start.4) | collective-permute-done | bytes 262176 | tf_op jit(solution)/shard_map/ppermute | solution.py:263
  289.9 0.6 shard_map.67
  290.6 0.1 collective-permute-start.5
  290.7 3.1 %collective-permute-done.6.outer = f32[32,2,8,128]{3,2,1,0:T(8,128)S(1)} collective-permute-done((f32[32,2,8,128]{3,2,1,0:T(8,128)S(1)}, f32[32,2,8,128]{3,2,1,0:T(8,128)S(1)}, u32[]{:S(2)}, u32[]{:S(2)}) %collective-permute-start.6) | collective-permute-done | bytes 262176 | tf_op jit(solution)/shard_map/ppermute | solution.py:263
  293.8 0.6 shard_map.68
  294.4 0.1 collective-permute-start.7
  294.5 0.0 collective-permute-done.3.outer
  294.5 1.6 shard_map.65
  296.1 2.5 collective-permute-done.5
  298.6 4.0 %collective-permute-done.7 = f32[256,256]{1,0:T(8,128)S(1)} collective-permute-done((f32[256,256]{1,0:T(8,128)S(1)}, f32[256,256]{1,0:T(8,128)S(1)}, u32[]{:S(2)}, u32[]{:S(2)}) %collective-permute-start.7) | collective-permute-done | bytes 262176 | tf_op jit(solution)/shard_map/ppermute | solution.py:273
  302.6 0.1 select_bitcast_fusion.5
  302.7 1.0 pad_maximum_fusion
  (4 shorter events, 0.1 us)
Async XLA Ops:
  4.8 11.6 %copy-start = (f32[1,256,256]{2,1,0:T(8,128)S(1)}, f32[1,256,256]{2,1,0:T(8,128)}, u32[]{:S(2)}) copy-start(f32[1,256,256]{2,1,0:T(8,128)} %param.8) | copy-start | bytes 786436
  4.8 11.6 %copy-start.1 = (f32[1,256,256]{2,1,0:T(8,128)S(1)}, f32[1,256,256]{2,1,0:T(8,128)}, u32[]{:S(2)}) copy-start(f32[1,256,256]{2,1,0:T(8,128)} %param.9) | copy-start | bytes 786436
  4.8 121.5 %all-to-all-start = ((f32[32,2,8,8,256]{4,3,2,1,0:T(8,128)}), f32[32,2,8,8,256]{4,3,2,1,0:T(8,128)}, u32[]{:S(2)}, u32[]{:S(2)}) async-start(f32[32,2,8,8,256]{4,3,2,1,0:T(8,128)} %copy_bitcast_fusion.1), calls=%async_computation | async-start | bytes 8388608 | tf_op jit(solution)/shard_map/all_to_all | solution.py:226
  16.4 97.6 %collective-permute-start = (f32[256,256]{1,0:T(8,128)S(1)}, f32[256,256]{1,0:T(8,128)S(1)}, u32[]{:S(2)}, u32[]{:S(2)}) collective-permute-start(f32[256,256]{1,0:T(8,128)S(1)} %bitcast_select_fusion.6), channel_id=1, source_target_pairs={{0,1},{1,0},{2,3},{3,2},{4,5},{5,4},{6,7},{7,6},{8,9},{9,8},{10,11... | collective-permute-start | bytes 786440 | tf_op jit(solution)/shard_map/ppermute | solution.py:224
  114.0 1.5 collective-permute-start.1
  115.6 10.2 %collective-permute-start.2 = (f32[256,256]{1,0:T(8,128)S(1)}, f32[256,256]{1,0:T(8,128)S(1)}, u32[]{:S(2)}, u32[]{:S(2)}) collective-permute-start(f32[256,256]{1,0:T(8,128)S(1)} %get-tuple-element.29), channel_id=1, source_target_pairs={{0,2},{2,4},{4,6},{1,3},{3,5},{5,7},{8,10},{10,12},{12,14},{9,11},... | collective-permute-start | bytes 786440 | tf_op jit(solution)/shard_map/ppermute | solution.py:233
  126.3 102.8 %all-to-all-start.1 = ((f32[256,2,8,256]{3,2,1,0:T(8,128)}), f32[256,2,8,256]{3,2,1,0:T(8,128)}, u32[]{:S(2)}, u32[]{:S(2)}) async-start(f32[256,2,8,256]{3,2,1,0:T(8,128)} %bitcast.76), calls=%async_computation.1 | async-start | bytes 8388608 | tf_op jit(solution)/shard_map/all_to_all | solution.py:242
  275.3 19.2 %collective-permute-start.3 = (f32[32,2,2,8,128]{4,3,2,1,0:T(8,128)S(1)}, f32[32,2,2,8,128]{4,3,2,1,0:T(8,128)S(1)}, u32[]{:S(2)}, u32[]{:S(2)}) collective-permute-start(f32[32,2,2,8,128]{4,3,2,1,0:T(8,128)S(1)} %get-tuple-element.24.far.near), channel_id=1, source_target_pairs={{0,2},{2,4},{3,1},{4,6},{5,3},{7,5},{8,10},{10,12},{11,9},{12,14},... | collective-permute-start | bytes 1572872 | tf_op jit(solution)/shard_map/ppermute | solution.py:264
  278.9 11.1 %collective-permute-start.4 = (f32[32,2,8,128]{3,2,1,0:T(8,128)S(1)}, f32[32,2,8,128]{3,2,1,0:T(8,128)S(1)}, u32[]{:S(2)}, u32[]{:S(2)}) collective-permute-start(f32[32,2,8,128]{3,2,1,0:T(8,128)S(1)} %get-tuple-element.33), channel_id=1, source_target_pairs={{1,3},{2,0},{3,5},{4,2},{5,7},{6,4},{9,11},{10,8},{11,13},{12,10},... | collective-permute-start | bytes 786440 | tf_op jit(solution)/shard_map/ppermute | solution.py:263
  281.3 12.5 %collective-permute-start.6 = (f32[32,2,8,128]{3,2,1,0:T(8,128)S(1)}, f32[32,2,8,128]{3,2,1,0:T(8,128)S(1)}, u32[]{:S(2)}, u32[]{:S(2)}) collective-permute-start(f32[32,2,8,128]{3,2,1,0:T(8,128)S(1)} %get-tuple-element.34), channel_id=1, source_target_pairs={{1,3},{2,0},{3,5},{4,2},{5,7},{6,4},{9,11},{10,8},{11,13},{12,10},... | collective-permute-start | bytes 786440 | tf_op jit(solution)/shard_map/ppermute | solution.py:263
  290.6 8.1 %collective-permute-start.5 = (f32[256,256]{1,0:T(8,128)S(1)}, f32[256,256]{1,0:T(8,128)S(1)}, u32[]{:S(2)}, u32[]{:S(2)}) collective-permute-start(f32[256,256]{1,0:T(8,128)S(1)} %shard_map.67), channel_id=1, source_target_pairs={{0,1},{1,0},{2,3},{3,2},{4,5},{5,4},{6,7},{7,6},{8,9},{9,8},{10,11... | collective-permute-start | bytes 786440 | tf_op jit(solution)/shard_map/ppermute | solution.py:273
  294.4 8.2 %collective-permute-start.7 = (f32[256,256]{1,0:T(8,128)S(1)}, f32[256,256]{1,0:T(8,128)S(1)}, u32[]{:S(2)}, u32[]{:S(2)}) collective-permute-start(f32[256,256]{1,0:T(8,128)S(1)} %shard_map.68), channel_id=1, source_target_pairs={{0,1},{1,0},{2,3},{3,2},{4,5},{5,4},{6,7},{7,6},{8,9},{9,8},{10,11... | collective-permute-start | bytes 786440 | tf_op jit(solution)/shard_map/ppermute | solution.py:273
